TPU v7x, 256 devices: a whole 4x4x8 slice. The times are simulated.
256 devices in a mesh: grp: 4 (over y), dev: 64 (over z, x, core).
Axes of the slice: x: 4, y: 4, z: 8, core: 2. Of those that a mesh axis runs over, the one named last changes fastest.
Arguments:
- pool_latent: bfloat16 [512, 256, 512], P(('grp', 'dev')), may hold values from -6 to 6
- pool_rope: bfloat16 [512, 64, 256], P(('grp', 'dev')), may hold values from -6 to 6
- q_nope: bfloat16 [1024, 16384], P(None, 'dev'), may hold values from -6 to 6
- q_rope: bfloat16 [1024, 8192], P(None, 'dev'), may hold values from -9 to 9
- w_uk: bfloat16 [512, 16384], P(None, 'dev'), may hold values from -0.25 to 0.25
- w_uv: bfloat16 [512, 16384], P(None, 'dev'), may hold values from -0.25 to 0.25
- w_o: bfloat16 [16384, 7168], P('dev'), may hold values from -0.046875 to 0.046875
- block_table: int32 [64, 8], replicated, may hold values from 0 to 511, as said below
- lengths: int32 [64], replicated, may hold values from 2 to 2048, as said below
- preempted: int32 [32], replicated, may hold values from 0 to 63, as said below
- assignment: int32 [32], replicated, may hold values from 0 to 3, as said below
Outputs:
- mixed: bfloat16 [1024, 7168], P('grp', 'dev')
Inputs may be any that keep to these rules, and one draw needn't show every extreme that they name: `preempted`: distinct slots. `assignment`: each group receives exactly 8 requests. `block_table`: every page number 0 to 511 appears exactly once in the table; page p lies on the device with index p // 2 along grp+dev, at position p % 2 there. For every group and every index along dev, exactly 1 of the pages listed for the slots of that group's requests lie on devices with that index along dev. `lengths`: in every draw all requests of one group hold more than (7) * 256 tokens.
All inputs are finite; a program needn't handle non-finite values.
Results may differ from a plain program's by a relative error of at most 0.015.
Values may be sent and summed in bfloat16 or wider, within the bound.
No kernel may reach another device: no remote copies, remote signals or barrier semaphores. Data moves between devices by JAX's collectives and lax.ppermute only.
A program may use at most 128 MiB of HBM per device.

v0:
```python
import math

import jax
import jax.numpy as jnp
from jax import lax
from jax.sharding import Mesh
from jax.sharding import PartitionSpec as P

DR = 64
DN = 128
DV = 128
DEV = ("dev_0", "dev_1", "dev_2")
GRP_DEV = ("grp", "dev_0", "dev_1", "dev_2")


NEG = -1e30


def sent_together(arrays, axis, split_dim, concat_dim, along):
    widths = [math.prod(a.shape[along:]) for a in arrays]
    both = jnp.concatenate(
        [a.reshape(*a.shape[:along], w) for a, w in zip(arrays, widths)], axis=along
    )
    filled = lax.all_to_all(both, axis, split_axis=split_dim, concat_axis=concat_dim, tiled=True)
    tiles = jnp.split(filled, [sum(widths[:k]) for k in range(1, len(widths))], axis=along)
    return tuple(
        (b.reshape(*filled.shape[:along], *a.shape[along:]) for a, b in zip(arrays, tiles))
    )


def summed_rows(so_far, axes):
    for axis in axes:
        so_far = lax.psum_scatter(so_far, axis, scatter_dimension=0, tiled=True)
    return so_far


def place_values(targets, values, length, dtype):
    return jnp.zeros((length + 1,), dtype).at[targets].set(values)[:length]


def local(
    pool_latent,
    pool_rope,
    q_nope,
    q_rope,
    w_uk,
    w_uv,
    w_o,
    block_table,
    lengths,
    preempted,
    assignment,
):
    groups = lax.axis_size("grp")
    columns = lax.axis_size(DEV)
    group = lax.axis_index("grp")
    column = lax.axis_index(DEV)
    pages_dev = pool_latent.shape[0]
    block = pool_latent.shape[1]
    latent_width = pool_latent.shape[2]
    rope_width = pool_rope.shape[1]
    requests = preempted.shape[0]
    blocks = block_table.shape[1]
    per_group = requests // groups
    group_pages = per_group * blocks
    per_column = group_pages // columns
    query_rows = q_nope.shape[0] // requests
    heads_dev = q_rope.shape[1] // rope_width
    scale = 1.0 / math.sqrt(DN + DR)
    slot_pages = block_table[preempted]
    slot_len = lengths[preempted]
    req_ids = jnp.arange(requests, dtype=jnp.int32)
    earlier = (assignment[:, None] == assignment[None, :]) & (req_ids[None, :] < req_ids[:, None])
    rank = jnp.sum(earlier.astype(jnp.int32), axis=1)
    entries = requests * blocks
    entry_ids = jnp.arange(entries, dtype=jnp.int32)
    entry_page = slot_pages.reshape(entries)
    entry_req = entry_ids // blocks
    entry_block = entry_ids % blocks
    entry_group = assignment[entry_req]
    holder = entry_page // pages_dev
    entry_row = holder // columns
    entry_col = holder % columns
    entry_local = entry_page % pages_dev
    entry_key = entry_col * groups + entry_group
    before = (entry_key[:, None] == entry_key[None, :]) & (entry_ids[None, :] < entry_ids[:, None])
    entry_slot = jnp.sum(before.astype(jnp.int32), axis=1)
    entry_pos = entry_col * per_column + entry_slot
    entry_valid = jnp.clip(slot_len[entry_req] - entry_block * block, 0, block)
    outgoing = groups * per_column
    sending = (entry_row == group) & (entry_col == column)
    send_target = jnp.where(sending, entry_group * per_column + entry_slot, outgoing)
    send_index = place_values(send_target, entry_local, outgoing, jnp.int32)
    send_live = place_values(send_target, jnp.ones((entries,), jnp.bool_), outgoing, jnp.bool_)
    zero = jnp.zeros((), pool_latent.dtype)
    out_latent = jnp.where(send_live[:, None, None], pool_latent[send_index], zero)
    out_rope = jnp.where(send_live[:, None, None], pool_rope[send_index], zero)
    got_latent, got_rope = sent_together((out_latent, out_rope), "grp", 0, 0, 1)
    mine = (entry_group == group) & (entry_col == column)
    source = place_values(jnp.where(mine, entry_slot, per_column), entry_row, per_column, jnp.int32)
    pick = source * per_column + jnp.arange(per_column, dtype=jnp.int32)
    own_latent = got_latent[pick]
    own_rope = got_rope[pick]
    in_group = entry_group == group
    pos_target = jnp.where(in_group, entry_pos, group_pages)
    page_req = place_values(pos_target, rank[entry_req], group_pages, jnp.int32)
    page_valid = place_values(pos_target, entry_valid, group_pages, jnp.int32)
    members = place_values(
        jnp.where(assignment == group, rank, per_group), req_ids, per_group, jnp.int32
    )
    rows = (
        members[:, None] * query_rows + jnp.arange(query_rows, dtype=jnp.int32)[None, :]
    ).reshape(-1)
    query_lo = q_nope[rows].reshape(per_group * query_rows, heads_dev, DN)
    query_hi = q_rope[rows].reshape(per_group, query_rows, heads_dev, rope_width)
    w_key = w_uk.reshape(latent_width, heads_dev, DN)
    q_lat = jnp.einsum("qhn,chn->qhc", query_lo, w_key, preferred_element_type=jnp.float32).astype(
        jnp.bfloat16
    )
    q_lat = q_lat.reshape(per_group, query_rows, heads_dev, latent_width)
    request_ids = jnp.arange(per_group, dtype=jnp.int32)
    token_ids = jnp.arange(block, dtype=jnp.int32)
    start_top = jnp.full((per_group, query_rows, heads_dev), NEG, jnp.float32)
    latent_piece = lax.all_gather(own_latent, DEV, axis=0, tiled=True)
    rope_piece = lax.all_gather(own_rope, DEV, axis=0, tiled=True)
    score = jnp.einsum(
        "pqhc,pkc->pqhk", q_lat[page_req], latent_piece, preferred_element_type=jnp.float32
    )
    score = score + jnp.einsum(
        "pqhr,prk->pqhk", query_hi[page_req], rope_piece, preferred_element_type=jnp.float32
    )
    score = score * scale
    live = token_ids[None, None, None, :] < page_valid[:, None, None, None]
    score = jnp.where(live, score, NEG)
    onehot = page_req[:, None] == request_ids[None, :]
    page_top = jnp.max(score, axis=3)
    piece_top = jnp.max(jnp.where(onehot[:, :, None, None], page_top[:, None], NEG), axis=0)
    top_new = jnp.maximum(start_top, piece_top)
    expo = jnp.where(live, jnp.exp(score - top_new[page_req][..., None]), 0.0)
    select = onehot.astype(jnp.float32)
    total_new = jnp.einsum(
        "pr,pqh->rqh", select, jnp.sum(expo, axis=3), precision=lax.Precision.HIGHEST
    )
    values = jnp.einsum(
        "pqhk,pkc->pqhc",
        expo.astype(jnp.bfloat16),
        latent_piece,
        preferred_element_type=jnp.float32,
    )
    acc_new = jnp.einsum("pr,pqhc->rqhc", select, values, precision=lax.Precision.HIGHEST)
    o_lat = (
        (acc_new / total_new[..., None])
        .astype(jnp.bfloat16)
        .reshape(per_group * query_rows, heads_dev, latent_width)
    )
    w_val = w_uv.reshape(latent_width, heads_dev, DV)
    heads_out = jnp.einsum("qhc,chv->qhv", o_lat, w_val, preferred_element_type=jnp.float32).astype(
        jnp.bfloat16
    )
    heads_out = heads_out.reshape(per_group * query_rows, heads_dev * DV)
    mixed = summed_rows(
        lax.dot_general(
            w_o, heads_out, (((0,), (1,)), ((), ())), preferred_element_type=jnp.float32
        ),
        DEV,
    )
    return mixed.T.astype(jnp.bfloat16)


def solution(mesh):
    split = Mesh(
        mesh.devices.reshape(mesh.shape["grp"], 8, 4, 2), ("grp", "dev_0", "dev_1", "dev_2")
    )
    return jax.shard_map(
        local,
        mesh=split,
        in_specs=(
            P(GRP_DEV, None, None),
            P(GRP_DEV, None, None),
            P(None, DEV),
            P(None, DEV),
            P(None, DEV),
            P(None, DEV),
            P(DEV, None),
            P(),
            P(),
            P(),
            P(),
        ),
        out_specs=P("grp", DEV),
        check_vma=False,
    )
```

profile of v0, /device:TPU:1, one launch (start us, length us, event | category | flops | bytes accessed | tf_op | source)
XLA Modules:
  0.0 423.7 jit_solution(13524470347480903052)
XLA Ops:
  8.3 1.8 fusion.55
  10.2 2.1 fusion.54
  14.5 4.3 %select_select_fusion.2 = s32[256,1]{0,1:T(1,128)S(1)} fusion(s32[]{:T(128)} %bitcast.25, s32[]{:T(128)} %bitcast.26, s32[]{:T(128)} %bitcast.27, s32[]{:T(128)} %bitcast.28, s32[]{:T(128)} %bitcast.29, s32[]{:T(128)} %bitcast.31, s32[]{:T(128)} %bitcast.30), kind=kLoop, calls=%fused_computation.134 | loop fusion | flops 5888 | bytes 1052 | tf_op jit(solution)/shard_map/gather | solution.py:80
  18.8 15.7 %fusion.32 = (s32[256]{0:T(256)S(1)}, s32[256]{0:T(256)S(1)}) fusion(s32[256]{0:T(256)S(1)} %get-tuple-element.31, pred[256]{0:T(512)(128)(4,1)S(1)} %compare_reduce_fusion, pred[256]{0:T(512)(128)(4,1)S(1)} %compare_reduce_fusion.1, pred[256]{0:T(512)(128)(4,1)S(1)} %compare_reduce_fusion.2, pred[256]{0:T(512)(128)(4,1)S(1)} %compare_reduce_fusion.3, ...), kind=kLoop, calls=%fused_computation.129 | loop fusion | flops 9728 | bytes 10596 | tf_op jit(solution)/shard_map/add | solution.py:85
  34.8 1.4 scatter_custom_fusion.4
  39.2 1.5 scatter_custom_fusion.3
  41.3 4.4 %maximum_bitcast_fusion = bf16[4,1,147456]{2,0,1:T(4,128)(2,1)S(1)} fusion(bf16[4,16384]{1,0:T(4,128)(2,1)S(1)} %broadcast_select_fusion.1, bf16[4,131072]{1,0:T(4,128)(2,1)S(1)} %broadcast_select_fusion), kind=kLoop, calls=%fused_computation.33 | loop fusion | flops 2359296 | bytes 2359296 | tf_op jit(solution)/shard_map/all_to_all | solution.py:24
  46.3 2.1 reduce.50
  48.4 2.2 reshape.904
  50.7 5.0 %all-to-all-start = ((bf16[4,2,73728]{2,1,0:T(2,128)(2,1)}), bf16[4,2,73728]{2,1,0:T(2,128)(2,1)}, u32[]{:S(2)}, u32[]{:S(2)}) async-start(bf16[4,2,73728]{2,1,0:T(2,128)(2,1)} %reshape.904), calls=%async_computation | async-start | bytes 2359296 | tf_op jit(solution)/shard_map/all_to_all | solution.py:24
  55.7 1.6 scatter_custom_fusion.5
  57.4 12.5 %all-to-all-done = bf16[4,2,73728]{2,1,0:T(2,128)(2,1)} async-done(((bf16[4,2,73728]{2,1,0:T(2,128)(2,1)}), bf16[4,2,73728]{2,1,0:T(2,128)(2,1)}, u32[]{:S(2)}, u32[]{:S(2)}) %all-to-all-start) | async-done | bytes 1179680 | tf_op jit(solution)/shard_map/all_to_all | solution.py:24
  69.9 2.7 reshape.905
  72.6 2.5 copy.99
  82.9 4.3 %select_select_fusion.1 = s32[256,1]{0,1:T(1,128)S(1)} fusion(s32[]{:T(128)} %bitcast.61, s32[]{:T(128)} %bitcast.62, s32[]{:T(128)} %bitcast.63, s32[]{:T(128)} %bitcast.64, s32[]{:T(128)} %bitcast.65, s32[]{:T(128)} %bitcast.67, s32[]{:T(128)} %bitcast.66), kind=kLoop, calls=%fused_computation.133 | loop fusion | flops 5888 | bytes 1052 | tf_op jit(solution)/shard_map/gather | solution.py:106
  88.0 15.5 %select_select_fusion.3 = s32[256]{0:T(256)S(1)} fusion(pred[256]{0:T(512)(128)(4,1)S(1)} %compare_reduce_fusion, pred[256]{0:T(512)(128)(4,1)S(1)} %compare_reduce_fusion.1, pred[256]{0:T(512)(128)(4,1)S(1)} %compare_reduce_fusion.2, pred[256]{0:T(512)(128)(4,1)S(1)} %compare_reduce_fusion.3, pred[256]{0:T(512)(128)(4,1)S(1)} %compare_reduce_fusion.4, ...), kind=kLoop, calls=%fused_computation.135 | loop fusion | flops 6400 | bytes 8548 | tf_op jit(solution)/shard_map/gather | solution.py:106
  105.2 2.7 gather_fusion.3
  110.1 4.3 %select_select_fusion = s32[256,1]{0,1:T(1,128)S(1)} fusion(s32[]{:T(128)} %bitcast.96, s32[]{:T(128)} %bitcast.97, s32[]{:T(128)} %bitcast.98, s32[]{:T(128)} %bitcast.99, s32[]{:T(128)} %bitcast.100, s32[]{:T(128)} %bitcast.102, s32[]{:T(128)} %bitcast.101), kind=kLoop, calls=%fused_computation.132 | loop fusion | flops 5888 | bytes 1052 | tf_op jit(solution)/shard_map/gather | solution.py:89
  115.2 15.5 %fusion.37 = s32[256]{0:T(256)S(1)} fusion(pred[256]{0:T(512)(128)(4,1)S(1)} %compare_reduce_fusion, pred[256]{0:T(512)(128)(4,1)S(1)} %compare_reduce_fusion.1, pred[256]{0:T(512)(128)(4,1)S(1)} %compare_reduce_fusion.2, pred[256]{0:T(512)(128)(4,1)S(1)} %compare_reduce_fusion.3, pred[256]{0:T(512)(128)(4,1)S(1)} %compare_reduce_fusion.4, ...), kind=kLoop, calls=%fused_computation.139 | loop fusion | flops 8704 | bytes 8548 | tf_op jit(solution)/shard_map/jit(clip)/min | solution.py:89
  130.7 1.4 scatter_custom_fusion.1
  132.4 49.0 %all-gather.3.cloned.1.call-done = bf16[64,256,512]{2,1,0:T(8,128)(2,1)} async-done(((bf16[1,256,512]{2,1,0:T(8,128)(2,1)}), bf16[64,256,512]{2,1,0:T(8,128)(2,1)}) %all-gather.3.cloned.1.call-update) | async-done | bytes 16777232 | tf_op jit(solution)/shard_map/all_gather | solution.py:124
  181.4 11.6 %fusion.2 = f32[64,32,2,256]{3,1,2,0:T(8,128)} fusion(bf16[64,32,2,512]{3,1,2,0:T(8,128)(2,1)} %gather_fusion.3, bf16[64,256,512]{2,1,0:T(8,128)(2,1)} %all-gather.3.cloned.1.call-done), kind=kOutput, calls=%fused_computation.17 | convolution fusion | flops 1073741824 | bytes 25165824 | tf_op jit(solution)/shard_map/pqhc,pkc->pqhk/dot_general | solution.py:126
  193.0 65.4 %all-gather.5.cloned.1.call-done = bf16[64,64,256]{2,1,0:T(8,128)(2,1)} async-done(((bf16[1,64,256]{2,1,0:T(8,128)(2,1)}), bf16[64,64,256]{2,1,0:T(8,128)(2,1)}) %all-gather.5.cloned.1.call-update) | async-done | bytes 2097168 | tf_op jit(solution)/shard_map/all_gather | solution.py:125
  258.4 5.7 %fusion.56 = (f32[64,32,2]{1,2,0:T(2,128)S(1)}, f32[64,32,2,256]{3,1,2,0:T(8,128)}) fusion(f32[64,32,2,256]{3,1,2,0:T(8,128)} %fusion.2, bf16[64,32,2,64]{3,1,2,0:T(8,128)(2,1)S(1)} %gather_fusion.7, bf16[64,64,256]{2,1,0:T(8,128)(2,1)} %all-gather.5.cloned.1.call-done, pred[64,256]{1,0:T(8,128)(4,1)S(1)} %iota_compare_fusion.1), kind=kOutput, calls=%fused_computation.171 | convolution fusion | flops 138407936 | bytes 11042816 | tf_op jit(solution)/shard_map/pqhr,prk->pqhk/dot_general | solution.py:129
  265.1 3.2 fusion.6
  268.5 9.6 %fusion = f32[64,32,2,512]{3,1,2,0:T(8,128)S(1)} fusion(bf16[64,256,512]{2,1,0:T(8,128)(2,1)} %all-gather.3.cloned.1.call-done, f32[64,32,2,256]{3,1,2,0:T(8,128)} %get-tuple-element.136, f32[64,32,2]{1,2,0:T(2,128)S(1)} %gather_fusion.8, pred[64,256]{1,0:T(8,128)(4,1)S(1)} %iota_compare_fusion.1), kind=kOutput, calls=%fused_computation.15 | convolution fusion | flops 1076887552 | bytes 29392896 | tf_op jit(solution)/shard_map/pqhk,pkc->pqhc/dot_general | solution.py:144
  278.1 7.5 %fusion.16 = bf16[8,32,2,512]{3,0,2,1:T(8,128)(2,1)S(1)} fusion(f32[64,32,2,512]{3,1,2,0:T(8,128)S(1)} %fusion, f32[8,32,2]{0,2,1:T(2,128)S(1)} %copy.61, s32[64]{0:T(128)S(1)} %get-tuple-element.37), kind=kOutput, calls=%fused_computation.31 | convolution fusion | flops 201851392 | bytes 8915200 | tf_op jit(solution)/shard_map/pr,pqhc->rqhc/dot_general | solution.py:150
  286.3 4.1 convolution_bitcast_fusion
  290.5 82.5 %reduce-scatter.8.cloned.1.call-done = f32[896,256]{0,1:T(8,128)} async-done(((f32[7168,256]{0,1:T(8,128)}), f32[896,256]{0,1:T(8,128)}) %reduce-scatter.8.cloned.1.call-update) | async-done | bytes 917520 | tf_op jit(solution)/shard_map/reduce_scatter | solution.py:33
  372.9 2.4 copy.69
  375.4 22.8 %reduce-scatter.10.cloned.1.call-done = f32[224,256]{1,0:T(8,128)} async-done(((f32[896,256]{1,0:T(8,128)}), f32[224,256]{1,0:T(8,128)}) %reduce-scatter.10.cloned.1.call-update) | async-done | bytes 229392
  398.2 17.2 %reduce-scatter.12.cloned.1.call-done = f32[112,256]{1,0:T(8,128)} async-done(((f32[224,256]{1,0:T(8,128)}), f32[112,256]{1,0:T(8,128)}) %reduce-scatter.12.cloned.1.call-update) | async-done | bytes 114704
  (114 shorter events, 25.1 us)
Async XLA Ops:
  6.5 31.2 %copy-start = (bf16[2,256,512]{2,1,0:T(8,128)(2,1)S(1)}, bf16[2,256,512]{2,1,0:T(8,128)(2,1)}, u32[]{:S(2)}) copy-start(bf16[2,256,512]{2,1,0:T(8,128)(2,1)} %param.11) | copy-start | bytes 1572868
  50.7 19.2 %all-to-all-start = ((bf16[4,2,73728]{2,1,0:T(2,128)(2,1)}), bf16[4,2,73728]{2,1,0:T(2,128)(2,1)}, u32[]{:S(2)}, u32[]{:S(2)}) async-start(bf16[4,2,73728]{2,1,0:T(2,128)(2,1)} %reshape.904), calls=%async_computation | async-start | bytes 2359296 | tf_op jit(solution)/shard_map/all_to_all | solution.py:24
  55.7 125.7 %all-gather.3.cloned.1.call-start = ((), (), s32[]{:S(2)}) async-start(), calls=%async_computation.4 | async-start | bytes 17039360 | tf_op jit(solution)/shard_map/all_gather | solution.py:124
  72.6 7.4 %copy-start.5 = (bf16[1024,256]{1,0:T(8,128)(2,1)S(1)}, bf16[1024,256]{1,0:T(8,128)(2,1)}, u32[]{:S(2)}) copy-start(bf16[1024,256]{1,0:T(8,128)(2,1)} %param.13) | copy-start | bytes 1572868
  75.1 1.0 copy-start.3
  75.1 6.1 %copy-start.6 = (bf16[1024,128]{1,0:T(8,128)(2,1)S(1)}, bf16[1024,128]{1,0:T(8,128)(2,1)}, u32[]{:S(2)}) copy-start(bf16[1024,128]{1,0:T(8,128)(2,1)} %param.14) | copy-start | bytes 786436
  75.2 29.7 %copy-start.7 = (bf16[512,256]{1,0:T(8,128)(2,1)S(1)}, bf16[512,256]{1,0:T(8,128)(2,1)}, u32[]{:S(2)}) copy-start(bf16[512,256]{1,0:T(8,128)(2,1)} %param.15) | copy-start | bytes 786436
  77.5 180.9 %all-gather.5.cloned.1.call-start = ((), (), s32[]{:S(2)}) async-start(), calls=%async_computation.5 | async-start | bytes 2129920 | tf_op jit(solution)/shard_map/all_gather | solution.py:125
  79.1 293.8 %reduce-scatter.8.cloned.1.call-start = ((), (), s32[]{:S(2)}) async-start(), calls=%async_computation.6 | async-start | bytes 8257536 | tf_op jit(solution)/shard_map/reduce_scatter | solution.py:33
  105.2 3.5 copy-start.2
  105.2 26.9 %copy-start.8 = (bf16[512,256]{1,0:T(8,128)(2,1)S(1)}, bf16[512,256]{1,0:T(8,128)(2,1)}, u32[]{:S(2)}) copy-start(bf16[512,256]{1,0:T(8,128)(2,1)} %param.16) | copy-start | bytes 786436
  278.1 8.1 %copy-start.4 = (bf16[256,7168]{1,0:T(8,128)(2,1)S(1)}, bf16[256,7168]{1,0:T(8,128)(2,1)}, u32[]{:S(2)}) copy-start(bf16[256,7168]{1,0:T(8,128)(2,1)} %param.17) | copy-start | bytes 11010052
  290.4 126.8 %copy-start.1 = (bf16[2,256,512]{2,1,0:T(8,128)(2,1)S(1)}, bf16[2,256,512]{2,1,0:T(8,128)(2,1)}, u32[]{:S(2)}) copy-start(bf16[2,256,512]{2,1,0:T(8,128)(2,1)} %param.11) | copy-start | bytes 1572868
  290.4 107.8 %reduce-scatter.10.cloned.1.call-start = ((), (), s32[]{:S(2)}) async-start(), calls=%async_computation.7 | async-start | bytes 1146880
  375.4 40.1 %reduce-scatter.12.cloned.1.call-start = ((), (), s32[]{:S(2)}) async-start(), calls=%async_computation.8 | async-start | bytes 344064
Sparse Core Ops, SparseCore 0:
  77.6 103.7 all-gather.2
  184.1 74.2 all-gather.4
  290.5 82.3 reduce-scatter.7
  375.5 22.6 reduce-scatter.9
  400.6 14.8 reduce-scatter.11
where the time goes:
time: 425 us; the launch traced here: 424 us
  waiting for transfers between devices  249 us (59%)
  other arithmetic  73.1 us (17%)
  local copies, waits for them, and re-layouts  42.8 us (10%)
  matrix products  39.3 us (9%)
  between operations  13.8 us (3%)
  starting transfers between devices  5.18 us (1%)
    reduce_scatter x1, waiting for transfers between devices, summed_rows(): so_far = lax.psum_scatter(so_far, axis, scatter_dimension=0, tiled=True)  82.5 us
    all_gather x1, waiting for transfers between devices, local(): rope_piece = lax.all_gather(own_rope, DEV, axis=0, tiled=True)  65.4 us
    all_gather x1, waiting for transfers between devices, local(): latent_piece = lax.all_gather(own_latent, DEV, axis=0, tiled=True)  49 us
    unnamed x7, waiting for transfers between devices  40.1 us
    gather x2, other arithmetic, local(): page_req = place_values(pos_target, rank[entry_req], group_pages, jnp.int32)  19.8 us
    add x1, other arithmetic, local(): entry_key = entry_col * groups + entry_group  15.7 us
    min x1, other arithmetic, local(): entry_valid = jnp.clip(slot_len[entry_req] - entry_block * block, 0, block)  15.5 us
    unnamed x28, local copies, waits for them, and re-layouts  13.8 us
  transfers between devices with their start and end apart: 6, of which 6 were waited for; matrix products, arithmetic and copies ran while one was open for 16% of the time, Pallas kernels for 0%

commit v1 on v0

v1 whole, which is shorter than its diff:
```python
import functools
import math

import jax
import jax.numpy as jnp
from jax import lax
from jax.experimental import pallas as pl
from jax.experimental.pallas import tpu as pltpu
from jax.sharding import Mesh
from jax.sharding import PartitionSpec as P

DR = 64
DN = 128
DV = 128
NEG = -1e30
NZ, NX, NC = 8, 4, 2
NXC = NX * NC
DEV = ("z", "x", "c")
GRP_DEV = ("grp", "z", "x", "c")
XC = ("x", "c")
SMEM = pltpu.SMEM
VMEM = pltpu.VMEM
F32 = jnp.float32
BF16 = jnp.bfloat16
NT = (((1,), (1,)), ((), ()))


def spec(space):
    return pl.BlockSpec(memory_space=space)


SEND, PICK, RANK, VALID, MEMBER, COUNT = 0, 4, 8, 16, 24, 32
META = 40


def index_kernel(ids, table, lengths, preempted, assignment, meta, *, groups, blocks, block, pages_dev):
    group, column = ids[0], ids[1]
    columns = NZ * NXC

    def clear(i, carry):
        meta[i] = 0
        return carry

    lax.fori_loop(0, META, clear, 0)

    def one_request(i, carry):
        slot = preempted[i]
        owner = assignment[i]
        length = lengths[slot]
        rank = meta[COUNT + owner]
        meta[COUNT + owner] = rank + 1
        mine = owner == group

        @pl.when(mine)
        def _():
            meta[MEMBER + rank] = i

        for b in range(blocks):
            page = table[slot, b]
            holder = page // pages_dev
            row = holder // columns
            col = holder % columns

            @pl.when((row == group) & (col == column))
            def _():
                meta[SEND + (owner - group + groups) % groups] = page % pages_dev

            @pl.when(mine & (col % NXC == column % NXC))
            def _():
                z = col // NXC
                meta[RANK + z] = rank
                meta[VALID + z] = jnp.clip(length - b * block, 0, block)

                @pl.when(col == column)
                def _():
                    meta[PICK] = (group - row + groups) % groups

        return carry

    lax.fori_loop(0, preempted.shape[0], one_request, 0)


def pack_kernel(meta, latent, rope, *rest):
    outs, sem = rest[:-1], rest[-1]
    block = latent.shape[1]
    half = rope.shape[1] // 2
    copies = []
    for k, out in enumerate(outs):
        page = meta[SEND + k]
        parts = (
            (latent.at[page], out.at[pl.ds(0, block), :]),
            (rope.at[page, pl.ds(0, half), :], out.at[pl.ds(block, half), pl.ds(0, block)]),
            (rope.at[page, pl.ds(half, half), :], out.at[pl.ds(block, half), pl.ds(block, block)]),
        )
        for j, (src, dst) in enumerate(parts):
            copies.append(pltpu.make_async_copy(src, dst, sem.at[k, j]))
    for copy in copies:
        copy.start()
    for copy in copies:
        copy.wait()


def pick_kernel(meta, *rest):
    sources, out, sem = rest[:-2], rest[-2], rest[-1]
    for k, source in enumerate(sources):

        @pl.when(meta[PICK] == k)
        def _():
            copy = pltpu.make_async_copy(source, out.at[0], sem)
            copy.start()
            copy.wait()


def query_kernel(meta, q_nope, q_rope, w_uk, out, rows):
    per_group = out.shape[0]
    q_rows = out.shape[1] // 2
    width = w_uk.shape[0]
    lane = lax.broadcasted_iota(jnp.int32, (q_rows, 2 * DR), 1)
    for r in range(per_group):
        start = pl.multiple_of(meta[MEMBER + r] * q_rows, q_rows)
        rows[r * q_rows : (r + 1) * q_rows, :] = q_nope[pl.ds(start, q_rows), :]
        hi = q_rope[pl.ds(start, q_rows), :]
        for h in range(2):
            live = (lane >= h * DR) & (lane < (h + 1) * DR)
            out[r, h * q_rows : (h + 1) * q_rows, width:] = jnp.where(live, hi, jnp.zeros_like(hi))
    for h in range(2):
        lat = lax.dot_general(
            rows[:, h * DN : (h + 1) * DN],
            w_uk[:, h * DN : (h + 1) * DN],
            NT,
            preferred_element_type=F32,
        ).astype(BF16)
        for r in range(per_group):
            out[r, h * q_rows : (h + 1) * q_rows, :width] = lat[r * q_rows : (r + 1) * q_rows, :]


def attention_kernel(meta, pages, *rest, scale):
    queries, w_uv = rest[:NXC], rest[NXC : 2 * NXC]
    keep, send, lse_keep, lse_send, acc, top, total = rest[2 * NXC :]
    per_group, heads_rows, width = acc.shape
    pair = heads_rows // NXC
    q_rows = pair // 2
    block = pages.shape[1] * 8 // 9
    half = pages.shape[1] - block

    acc[...] = jnp.zeros_like(acc)
    top[...] = jnp.full_like(top, NEG)
    total[...] = jnp.zeros_like(total)

    def one_page(z, carry):
        r = meta[RANK + z]
        valid = meta[VALID + z]

        @pl.when(valid > 0)
        def _():
            latent = pages[z, :block, :]
            tail = pages[z, block:, :]
            rope = jnp.concatenate([tail[:, :block], tail[:, block:]], axis=0)
            rope = jnp.concatenate([rope, rope], axis=0)
            query = jnp.concatenate([q[r] for q in queries], axis=0)
            score = lax.dot_general(query[:, :width], latent, NT, preferred_element_type=F32)
            score = score + jnp.dot(query[:, width:], rope, preferred_element_type=F32)
            token = lax.broadcasted_iota(jnp.int32, score.shape, 1)
            live = token < valid
            score = jnp.where(live, score * scale, NEG)
            old = top[r][:, :1]
            new = jnp.maximum(old, jnp.max(score, axis=1, keepdims=True))
            expo = jnp.where(live, jnp.exp(score - new), 0.0)
            fade = jnp.exp(old - new)
            top[r] = jnp.broadcast_to(new, top.shape[1:])
            total[r] = total[r] * fade + jnp.sum(expo, axis=1, keepdims=True)
            acc[r] = acc[r] * fade + jnp.dot(
                expo.astype(BF16), latent, preferred_element_type=F32
            )

        return carry

    lax.fori_loop(0, NZ, one_page, 0)

    for s in range(NXC):
        out, lse = (keep, lse_keep) if s % 2 == 0 else (send, lse_send)
        for h in range(2):
            lo = s * pair + h * q_rows
            rows = per_group * q_rows
            weight = total[:, lo : lo + q_rows, :].reshape(rows, total.shape[2])
            high = top[:, lo : lo + q_rows, :].reshape(rows, top.shape[2])
            value = acc[:, lo : lo + q_rows, :].reshape(rows, width)
            some = weight > 0.0
            safe = jnp.where(some, weight, 1.0)
            value = (value / safe[:, :1]).astype(BF16)
            head = jnp.dot(value, w_uv[s][:, h * DV : (h + 1) * DV], preferred_element_type=F32)
            out[s // 2, :, h * DV : (h + 1) * DV] = head.astype(BF16)
            stat = jnp.where(some, high + jnp.log(safe), NEG)
            lse[(s // 2) * 2 + h : (s // 2) * 2 + h + 1, :] = stat.T[:1, :]


def output_kernel(*refs):
    weights, heads, out = refs[:NXC], refs[NXC:-1], refs[-1]
    mixed = None
    for w, h in zip(weights, heads):
        term = lax.dot_general(w[...], h[...], NT, preferred_element_type=F32)
        mixed = term if mixed is None else mixed + term
    out[...] = mixed.astype(BF16)


def sent(x, axis, size, k):
    return lax.ppermute(x, axis, [(i, i ^ k) for i in range(size)])


def gathered(x):
    near = [x] + [sent(x, "x", NX, k) for k in range(1, NX)]
    far = [sent(a, "c", NC, 1) for a in near]
    return [a for pair in zip(near, far) for a in pair]


def over_rows(stat):
    return jnp.repeat(stat.T, DV, axis=1)


def merged(parts, stats):
    high = functools.reduce(jnp.maximum, stats)
    shares = [jnp.exp(s - high) for s in stats]
    whole = functools.reduce(jnp.add, shares)
    out = sum(over_rows(w / whole) * p.astype(F32) for w, p in zip(shares, parts))
    return out.astype(BF16), high + jnp.log(whole)


def local(
    pool_latent,
    pool_rope,
    q_nope,
    q_rope,
    w_uk,
    w_uv,
    w_o,
    block_table,
    lengths,
    preempted,
    assignment,
):
    groups = lax.axis_size("grp")
    group = lax.axis_index("grp")
    column = lax.axis_index(DEV)
    place = lax.axis_index(XC)
    pages_dev, block, width = pool_latent.shape
    requests = preempted.shape[0]
    blocks = block_table.shape[1]
    per_group = requests // groups
    query_rows = q_nope.shape[0] // requests
    rows = per_group * query_rows
    pair = 2 * query_rows
    scale = 1.0 / math.sqrt(DN + DR)
    page_rows = block + DR // 2

    ids = jnp.stack([group, column]).astype(jnp.int32)
    meta = pl.pallas_call(
        functools.partial(
            index_kernel, groups=groups, blocks=blocks, block=block, pages_dev=pages_dev
        ),
        out_shape=jax.ShapeDtypeStruct((META,), jnp.int32),
        in_specs=[spec(SMEM)] * 5,
        out_specs=spec(SMEM),
        name="index",
    )(ids, block_table, lengths, preempted, assignment)

    page_type = jax.ShapeDtypeStruct((page_rows, width), BF16)
    packed = pl.pallas_call(
        pack_kernel,
        out_shape=[page_type] * groups,
        in_specs=[spec(SMEM)] + [spec(pl.ANY)] * 2,
        out_specs=[spec(pl.ANY)] * groups,
        scratch_shapes=[pltpu.SemaphoreType.DMA((groups, 3))],
        name="pack",
    )(meta, pool_latent, pool_rope)
    arrived = [packed[0]] + [
        lax.ppermute(packed[k], "grp", [(i, (i + k) % groups) for i in range(groups)])
        for k in range(1, groups)
    ]
    own = pl.pallas_call(
        pick_kernel,
        out_shape=jax.ShapeDtypeStruct((1, page_rows, width), BF16),
        in_specs=[spec(SMEM)] + [spec(pl.ANY)] * groups,
        out_specs=spec(pl.ANY),
        scratch_shapes=[pltpu.SemaphoreType.DMA],
        name="pick",
    )(meta, *arrived)
    pages = lax.all_gather(own, "z", axis=0, tiled=True)

    query = pl.pallas_call(
        query_kernel,
        out_shape=jax.ShapeDtypeStruct((per_group, pair, width + 2 * DR), BF16),
        in_specs=[spec(SMEM)] + [spec(VMEM)] * 3,
        out_specs=spec(VMEM),
        scratch_shapes=[VMEM((rows, 2 * DN), BF16)],
        name="query",
    )(meta, q_nope, q_rope, w_uk)
    queries = gathered(query)
    values = gathered(w_uv)

    half_type = jax.ShapeDtypeStruct((NX, rows, 2 * DV), BF16)
    stat_type = jax.ShapeDtypeStruct((NXC, rows), F32)
    keep, send, lse_keep, lse_send = pl.pallas_call(
        functools.partial(attention_kernel, scale=scale),
        out_shape=[half_type, half_type, stat_type, stat_type],
        in_specs=[spec(SMEM)] + [spec(VMEM)] * (1 + 2 * NXC),
        out_specs=[spec(VMEM)] * 4,
        scratch_shapes=[
            VMEM((per_group, NXC * pair, width), F32),
            VMEM((per_group, NXC * pair, 128), F32),
            VMEM((per_group, NXC * pair, 128), F32),
        ],
        compiler_params=pltpu.CompilerParams(vmem_limit_bytes=48 << 20),
        name="attention",
    )(meta, pages, *queries, *values)

    w_cols = w_o.T.reshape(NZ, NXC, w_o.shape[1] // (NZ * NXC), w_o.shape[0])
    weights = []
    for s in range(NXC):
        part = lax.dynamic_index_in_dim(w_cols, place ^ s, 1, keepdims=False)
        part = part.reshape(-1, w_o.shape[0])
        weights.append(sent(part, XC, NXC, s) if s else part)

    got = sent(send, "c", NC, 1)
    lse_got = sent(lse_send, "c", NC, 1)
    chip = [
        merged(
            (keep[k], got[k]), (lse_keep[2 * k : 2 * k + 2], lse_got[2 * k : 2 * k + 2])
        )
        for k in range(NX)
    ]
    parts, stats = [chip[0][0]], [chip[0][1]]
    for k in range(1, NX):
        parts.append(sent(chip[k][0], "x", NX, k))
        stats.append(sent(chip[k][1], "x", NX, k))
    heads, _ = merged(parts, stats)
    all_heads = gathered(heads)

    mixed = pl.pallas_call(
        output_kernel,
        out_shape=jax.ShapeDtypeStruct((weights[0].shape[0], rows), BF16),
        in_specs=[spec(VMEM)] * (2 * NXC),
        out_specs=spec(VMEM),
        name="output",
    )(*weights, *all_heads)
    mixed = lax.all_to_all(mixed, "z", split_axis=0, concat_axis=0, tiled=True)
    mixed = mixed.reshape(NZ, -1, rows).astype(F32).sum(axis=0)
    return mixed.T.astype(BF16)


def solution(mesh):
    split = Mesh(mesh.devices.reshape(mesh.shape["grp"], NZ, NX, NC), GRP_DEV)
    return jax.shard_map(
        local,
        mesh=split,
        in_specs=(
            P(GRP_DEV, None, None),
            P(GRP_DEV, None, None),
            P(None, DEV),
            P(None, DEV),
            P(None, DEV),
            P(None, DEV),
            P(DEV, None),
            P(),
            P(),
            P(),
            P(),
        ),
        out_specs=P("grp", DEV),
        check_vma=False,
    )
```

time: 425 us -> 289 us (0.68)
  waiting for transfers between devices: 249 us -> 97 us
  Pallas kernels: 0 us -> 77.9 us
  other arithmetic: 73.1 us -> 3.87 us
  matrix products: 39.3 us -> 0 us
  starting transfers between devices: 5.18 us -> 42.8 us
  blocking collectives: 0 us -> 24.7 us
  local copies, waits for them, and re-layouts: 42.8 us -> 28.4 us
    all_gather x2 -> x1, waiting for transfers between devices: 114 us -> 0.01 us  [local(): pages = lax.all_gather(own, 'z', axis=0, tiled=True)]
    ppermute x0 -> x39, waiting for transfers between devices: none -> 97 us  [the longest x36 85.1 us: sent(): return lax.ppermute(x, axis, [(i, i ^ k) for i in range(size)])]
    reduce_scatter x1 -> x0, waiting for transfers between devices: 82.5 us -> none  [summed_rows(): so_far = lax.psum_scatter(so_far, axis, scatter_dimension=0, tiled=True)]
    pallas_call x0 -> x6, Pallas kernels: none -> 77.9 us  [the longest x1 37.7 us: local(): pl.pallas_call(pack_kernel, out_shape=[page_type] * groups, in_specs=[spe...]
    ppermute x0 -> x39, starting transfers between devices: none -> 42.8 us  [the longest x36 36.9 us: sent(): return lax.ppermute(x, axis, [(i, i ^ k) for i in range(size)])]
    unnamed x7 -> x1, waiting for transfers between devices: 40.1 us -> 0.02 us
    dot_general x8 -> x0, matrix products: 39.3 us -> none  [the longest x1 11.6 us: local(): jnp.einsum('pqhc,pkc->pqhk', q_lat[page_req], latent_piece, preferred_ele...]
    gather x33 -> x0, other arithmetic: 29.3 us -> none  [the longest x2 19.8 us: local(): page_req = place_values(pos_target, rank[entry_req], group_pages, jnp.int32)]
  transfers between devices with their start and end apart: 6 -> 40, of which waited for: 6 -> 14; matrix products, arithmetic and copies ran while one was open for 16% -> 6% of each run, Pallas kernels for 0% -> 1%
where the time goes in v1:
time: 289 us
  waiting for transfers between devices  97 us (34%)
  Pallas kernels  77.9 us (27%)
  starting transfers between devices  42.8 us (15%)
  local copies, waits for them, and re-layouts  28.4 us (10%)
  blocking collectives  24.7 us (9%)
  between operations  13.9 us (5%)
  other arithmetic  3.87 us (1%)
    ppermute x36, waiting for transfers between devices, sent(): return lax.ppermute(x, axis, [(i, i ^ k) for i in range(size)])  85.1 us
    pallas_call x1, Pallas kernels, local(): pl.pallas_call(pack_kernel, out_shape=[page_type] * groups, in_specs=[spe...  37.7 us
    ppermute x36, starting transfers between devices, sent(): return lax.ppermute(x, axis, [(i, i ^ k) for i in range(size)])  36.9 us
    all_to_all x1, blocking collectives, local(): mixed = lax.all_to_all(mixed, 'z', split_axis=0, concat_axis=0, tiled=True)  24.7 us
    unnamed x80, local copies, waits for them, and re-layouts  19 us
    pallas_call x1, Pallas kernels, local(): pl.pallas_call(functools.partial(attention_kernel, scale=scale), out_shap...  14.5 us
    ppermute x3, waiting for transfers between devices, local(): lax.ppermute(packed[k], 'grp', [(i, (i + k) % groups) for i in range(grou...  11.9 us
    pallas_call x1, Pallas kernels, local(): pl.pallas_call(pick_kernel, out_shape=jax.ShapeDtypeStruct((1, page_rows,...  10.7 us
  transfers between devices with their start and end apart: 40, of which 14 were waited for; matrix products, arithmetic and copies ran while one was open for 6% of the time, Pallas kernels for 1%

profile of v1, /device:TPU:1, one launch (start us, length us, event | category | flops | bytes accessed | tf_op | source)
XLA Modules:
  0.0 288.5 jit_solution(13787937653677755462)
XLA Ops:
  8.5 8.5 %index.1.meta = s32[40]{0:T(128)} custom-call(s32[2]{0:T(128)} %pad_add_fusion.ids, s32[64,8]{1,0:T(8,128)} %copy.48.table, s32[64]{0:T(128)} %lengths.1, s32[32]{0:T(128)} %preempted.1, s32[32]{0:T(128)} %assignment.1), custom_call_target="tpu_custom_call" | custom-call | tf_op jit(solution)/shard_map/index/pallas_call | solution.py:256
  17.0 37.7 %pack.1 = (bf16[288,512]{1,0:T(8,128)(2,1)}, bf16[288,512]{1,0:T(8,128)(2,1)}, bf16[288,512]{1,0:T(8,128)(2,1)}, bf16[288,512]{1,0:T(8,128)(2,1)}) custom-call(s32[40]{0:T(128)} %index.1.meta, bf16[2,256,512]{2,1,0:T(8,128)(2,1)} %latent.1, bf16[2,64,256]{2,1,0:T(8,128)(2,1)} %rope.1), custom_call_target="tpu_custom_call" | custom-call | tf_op jit(solution)/shard_map/pack/pallas_call | solution.py:267
  54.7 2.2 collective-permute-start.7
  56.9 2.6 collective-permute-start.8
  60.6 2.7 collective-permute-done.7.rest_1_
  63.3 9.2 %collective-permute-done.8.rest_2_ = bf16[288,512]{1,0:T(8,128)(2,1)S(1)} collective-permute-done((bf16[288,512]{1,0:T(8,128)(2,1)}, bf16[288,512]{1,0:T(8,128)(2,1)S(1)}, u32[]{:S(2)}, u32[]{:S(2)}) %collective-permute-start.8) | collective-permute-done | bytes 294944 | tf_op jit(solution)/shard_map/ppermute | solution.py:276
  73.3 10.7 %pick.1 = bf16[1,288,512]{2,1,0:T(8,128)(2,1)} custom-call(s32[40]{0:T(128)} %index.1.meta, bf16[288,512]{1,0:T(8,128)(2,1)} %get-tuple-element.13.rest_0_, bf16[288,512]{1,0:T(8,128)(2,1)} %copy-done.20, bf16[288,512]{1,0:T(8,128)(2,1)} %copy-done.21, bf16[288,512]{1,0:T(8,128)(2,1)} %copy-done.22), custom_call_target="tpu_custom_call" | custom-call | tf_op jit(solution)/shard_map/pick/pallas_call | solution.py:279
  85.3 2.3 query.1.rest_0_
  87.9 2.7 collective-permute-start.13
  93.5 33.1 %collective-permute-done.20.rest_12_ = bf16[512,256]{1,0:T(8,128)(2,1)S(1)} collective-permute-done((bf16[512,256]{1,0:T(8,128)(2,1)S(1)}, bf16[512,256]{1,0:T(8,128)(2,1)S(1)}, u32[]{:S(2)}, u32[]{:S(2)}) %collective-permute-start.20) | collective-permute-done | bytes 262176 | tf_op jit(solution)/shard_map/ppermute | solution.py:207
  126.5 2.5 collective-permute-start.17
  129.1 2.1 collective-permute-done.22.rest_14_
  131.2 3.3 %collective-permute-start.19 = (bf16[512,256]{1,0:T(8,128)(2,1)S(1)}, bf16[512,256]{1,0:T(8,128)(2,1)S(1)}, u32[]{:S(2)}, u32[]{:S(2)}) collective-permute-start(bf16[512,256]{1,0:T(8,128)(2,1)S(1)} %collective-permute-done.18.rest_10_), channel_id=1, source_target_pairs={{0,1},{1,0},{2,3},{3,2},{4,5},{5,4},{6,7},{7,6},{8,9},{9,8},{10,11... | collective-permute-start | bytes 786440 | tf_op jit(solution)/shard_map/ppermute | solution.py:207
  137.2 3.3 %collective-permute-done.21.rest_13_ = bf16[512,256]{1,0:T(8,128)(2,1)S(1)} collective-permute-done((bf16[512,256]{1,0:T(8,128)(2,1)S(1)}, bf16[512,256]{1,0:T(8,128)(2,1)S(1)}, u32[]{:S(2)}, u32[]{:S(2)}) %collective-permute-start.21) | collective-permute-done | bytes 262176 | tf_op jit(solution)/shard_map/ppermute | solution.py:207
  149.3 14.5 %attention.1 = (bf16[4,256,256]{2,1,0:T(8,128)(2,1)S(1)}, bf16[4,256,256]{2,1,0:T(8,128)(2,1)S(1)}, f32[8,256]{1,0:T(8,128)S(1)}, f32[8,256]{1,0:T(8,128)}) custom-call(s32[40]{0:T(128)S(1)} %copy-done.10, bf16[8,288,512]{2,1,0:T(8,128)(2,1)} %all-gather.2.cloned.1.call-done.pages, bf16[8,64,640]{2,1,0:T(8,128)(2,1)S(1)} %copy-done, ...), custom_call_target="tpu_custom_call" | custom-call | tf_op jit(solution)/shard_map/attention/pallas_call | solution.py:302
  164.7 6.0 %copy.47 = bf16[256,7168]{0,1:T(8,128)(2,1)} copy(bf16[256,7168]{1,0:T(8,128)(2,1)} %param.17) | data formatting | bytes 7340032 | tf_op args[6]
  171.2 2.0 collective-permute-start.26
  173.2 1.8 collective-permute-start.27
  175.0 3.7 %constant_dynamic-slice_fusion = (bf16[8,1,112,256]{3,2,1,0:T(8,128)(2,1)S(1)}, bf16[8,1,112,256]{3,2,1,0:T(8,128)(2,1)}, bf16[8,1,112,256]{3,2,1,0:T(8,128)(2,1...) fusion(bf16[8,8,112,256]{3,2,1,0:T(8,128)(2,1)} %bitcast.149, ...), kind=kLoop, calls=%fused_computation.46 | loop fusion | bytes 7340064 | tf_op jit(solution)/shard_map/jit(dynamic_index_in_dim)/dynamic_slice | solution.py:319
  186.4 1.6 collective-permute-start.2
  188.0 1.9 collective-permute-start.3
  189.8 2.6 collective-permute-done.1.refs_2_
  196.0 2.5 collective-permute-done.30
  198.5 1.8 collective-permute-start.31
  201.3 28.7 %collective-permute-done.31 = bf16[256,256]{1,0:T(8,128)(2,1)} collective-permute-done((bf16[256,256]{1,0:T(8,128)(2,1)}, bf16[256,256]{1,0:T(8,128)(2,1)}, u32[]{:S(2)}, u32[]{:S(2)}) %collective-permute-start.31) | collective-permute-done | bytes 131104 | tf_op jit(solution)/shard_map/ppermute | solution.py:207
  230.0 3.4 %collective-permute-start.6 = (bf16[896,256]{1,0:T(8,128)(2,1)S(1)}, bf16[896,256]{1,0:T(8,128)(2,1)S(1)}, u32[]{:S(2)}, u32[]{:S(2)}) collective-permute-start(bf16[896,256]{1,0:T(8,128)(2,1)S(1)} %bitcast.164), channel_id=1, source_target_pairs={{0,7},{1,6},{2,5},{3,4},{4,3},{5,2},{6,1},{7,0},{8,15},{9,14},{10,... | collective-permute-start | bytes 1376264 | tf_op jit(solution)/shard_map/ppermute | solution.py:207
  236.7 2.4 collective-permute-start.35
  240.5 1.6 collective-permute-done.33.refs_10_
  242.1 3.0 %collective-permute-done.35.refs_12_ = bf16[256,256]{1,0:T(8,128)(2,1)S(1)} collective-permute-done((bf16[256,256]{1,0:T(8,128)(2,1)S(1)}, bf16[256,256]{1,0:T(8,128)(2,1)S(1)}, u32[]{:S(2)}, u32[]{:S(2)}) %collective-permute-start.35) | collective-permute-done | bytes 131104 | tf_op jit(solution)/shard_map/ppermute | solution.py:207
  245.2 4.9 %collective-permute-done.37.refs_14_ = bf16[256,256]{1,0:T(8,128)(2,1)S(1)} collective-permute-done((bf16[256,256]{1,0:T(8,128)(2,1)S(1)}, bf16[256,256]{1,0:T(8,128)(2,1)S(1)}, u32[]{:S(2)}, u32[]{:S(2)}) %collective-permute-start.37) | collective-permute-done | bytes 131104 | tf_op jit(solution)/shard_map/ppermute | solution.py:207
  252.1 4.2 %output.1 = bf16[896,256]{1,0:T(8,128)(2,1)} custom-call(bf16[896,256]{1,0:T(8,128)(2,1)} %bitcast.150, bf16[896,256]{1,0:T(8,128)(2,1)} %copy-done.17, bf16[896,256]{1,0:T(8,128)(2,1)} %collective-permute-done.1.refs_2_, bf16[896,256]{1,0:T(8,128)(2,1)} %copy-done.18, bf16[896,256]{1,0:T(8,128)(2,1)} %collective-permute-done.3.refs_4_, ...), custom_call_target="tpu_custom_call" | custom-call | tf_op jit(solution)/shard_map/output/pallas_call | solution.py:338
  256.3 24.7 %all_to_all.9 = bf16[8,112,256]{2,1,0:T(8,128)(2,1)S(1)} all-to-all(bf16[8,112,256]{2,1,0:T(8,128)(2,1)} %bitcast.151), channel_id=1, replica_groups=mesh['grp'=4,'z'=8,'x'=4,'c'=2] {'z'}, dimensions={0} | all-to-all | bytes 917504 | tf_op jit(solution)/shard_map/all_to_all | solution.py:345
  (168 shorter events, 40.2 us)
Async XLA Ops:
  6.5 137.8 %all-gather.2.cloned.1.call-start = ((), (), s32[]{:S(2)}) async-start(), calls=%async_computation.1 | async-start | bytes 2654208 | tf_op jit(solution)/shard_map/all_gather | solution.py:287
  54.7 8.5 %collective-permute-start.7 = (bf16[288,512]{1,0:T(8,128)(2,1)}, bf16[288,512]{1,0:T(8,128)(2,1)S(1)}, u32[]{:S(2)}, u32[]{:S(2)}) collective-permute-start(bf16[288,512]{1,0:T(8,128)(2,1)} %get-tuple-element.14), channel_id=1, source_target_pairs={{0,64},{64,128},{128,192},{192,0},{1,65},{65,129},{129,193},{193,1... | collective-permute-start | bytes 884744 | tf_op jit(solution)/shard_map/ppermute | solution.py:276
  56.9 15.6 %collective-permute-start.8 = (bf16[288,512]{1,0:T(8,128)(2,1)}, bf16[288,512]{1,0:T(8,128)(2,1)S(1)}, u32[]{:S(2)}, u32[]{:S(2)}) collective-permute-start(bf16[288,512]{1,0:T(8,128)(2,1)} %get-tuple-element.15), channel_id=1, source_target_pairs={{0,128},{64,192},{128,0},{192,64},{1,129},{65,193},{129,1},{193,65... | collective-permute-start | bytes 884744 | tf_op jit(solution)/shard_map/ppermute | solution.py:276
  59.6 12.9 %collective-permute-start.9 = (bf16[288,512]{1,0:T(8,128)(2,1)}, bf16[288,512]{1,0:T(8,128)(2,1)S(1)}, u32[]{:S(2)}, u32[]{:S(2)}) collective-permute-start(bf16[288,512]{1,0:T(8,128)(2,1)} %get-tuple-element.16), channel_id=1, source_target_pairs={{0,192},{64,0},{128,64},{192,128},{1,193},{65,1},{129,65},{193,129... | collective-permute-start | bytes 884744 | tf_op jit(solution)/shard_map/ppermute | solution.py:276
  84.0 8.8 %collective-permute-start.18 = (bf16[512,256]{1,0:T(8,128)(2,1)}, bf16[512,256]{1,0:T(8,128)(2,1)S(1)}, u32[]{:S(2)}, u32[]{:S(2)}) collective-permute-start(bf16[512,256]{1,0:T(8,128)(2,1)} %rest_8_.1), channel_id=1, source_target_pairs={{0,2},{2,0},{4,6},{6,4},{1,3},{3,1},{5,7},{7,5},{8,10},{10,8},{12,... | collective-permute-start | bytes 786440 | tf_op jit(solution)/shard_map/ppermute | solution.py:207
  87.7 47.6 %collective-permute-start.11 = (bf16[8,64,640]{2,1,0:T(8,128)(2,1)}, bf16[8,64,640]{2,1,0:T(8,128)(2,1)S(1)}, u32[]{:S(2)}, u32[]{:S(2)}) collective-permute-start(bf16[8,64,640]{2,1,0:T(8,128)(2,1)} %query.1.rest_0_), channel_id=1, source_target_pairs={{0,2},{2,0},{4,6},{6,4},{1,3},{3,1},{5,7},{7,5},{8,10},{10,8},{12,... | collective-permute-start | bytes 1966088 | tf_op jit(solution)/shard_map/ppermute | solution.py:207
  87.9 47.8 %collective-permute-start.13 = (bf16[8,64,640]{2,1,0:T(8,128)(2,1)}, bf16[8,64,640]{2,1,0:T(8,128)(2,1)S(1)}, u32[]{:S(2)}, u32[]{:S(2)}) collective-permute-start(bf16[8,64,640]{2,1,0:T(8,128)(2,1)} %query.1.rest_0_), channel_id=1, source_target_pairs={{0,4},{2,6},{4,0},{6,2},{1,5},{3,7},{5,1},{7,3},{8,12},{10,14},{12... | collective-permute-start | bytes 1966088 | tf_op jit(solution)/shard_map/ppermute | solution.py:207
  90.7 45.2 %collective-permute-start.15 = (bf16[8,64,640]{2,1,0:T(8,128)(2,1)}, bf16[8,64,640]{2,1,0:T(8,128)(2,1)S(1)}, u32[]{:S(2)}, u32[]{:S(2)}) collective-permute-start(bf16[8,64,640]{2,1,0:T(8,128)(2,1)} %query.1.rest_0_), channel_id=1, source_target_pairs={{0,6},{2,4},{4,2},{6,0},{1,7},{3,5},{5,3},{7,1},{8,14},{10,12},{12... | collective-permute-start | bytes 1966088 | tf_op jit(solution)/shard_map/ppermute | solution.py:207
  91.5 35.0 %collective-permute-start.20 = (bf16[512,256]{1,0:T(8,128)(2,1)S(1)}, bf16[512,256]{1,0:T(8,128)(2,1)S(1)}, u32[]{:S(2)}, u32[]{:S(2)}) collective-permute-start(bf16[512,256]{1,0:T(8,128)(2,1)S(1)} %copy-done.1), channel_id=1, source_target_pairs={{0,4},{2,6},{4,0},{6,2},{1,5},{3,7},{5,1},{7,3},{8,12},{10,14},{12... | collective-permute-start | bytes 786440 | tf_op jit(solution)/shard_map/ppermute | solution.py:207
  92.8 38.4 %collective-permute-start.22 = (bf16[512,256]{1,0:T(8,128)(2,1)S(1)}, bf16[512,256]{1,0:T(8,128)(2,1)S(1)}, u32[]{:S(2)}, u32[]{:S(2)}) collective-permute-start(bf16[512,256]{1,0:T(8,128)(2,1)S(1)} %copy-done.1), channel_id=1, source_target_pairs={{0,6},{2,4},{4,2},{6,0},{1,7},{3,5},{5,3},{7,1},{8,14},{10,12},{12... | collective-permute-start | bytes 786440 | tf_op jit(solution)/shard_map/ppermute | solution.py:207
  126.5 8.0 %collective-permute-start.17 = (bf16[512,256]{1,0:T(8,128)(2,1)S(1)}, bf16[512,256]{1,0:T(8,128)(2,1)S(1)}, u32[]{:S(2)}, u32[]{:S(2)}) collective-permute-start(bf16[512,256]{1,0:T(8,128)(2,1)S(1)} %copy-done.1), channel_id=1, source_target_pairs={{0,1},{1,0},{2,3},{3,2},{4,5},{5,4},{6,7},{7,6},{8,9},{9,8},{10,11... | collective-permute-start | bytes 786440 | tf_op jit(solution)/shard_map/ppermute | solution.py:207
  135.2 8.2 %collective-permute-start.10 = (bf16[8,64,640]{2,1,0:T(8,128)(2,1)}, bf16[8,64,640]{2,1,0:T(8,128)(2,1)S(1)}, u32[]{:S(2)}, u32[]{:S(2)}) collective-permute-start(bf16[8,64,640]{2,1,0:T(8,128)(2,1)} %query.1.rest_0_), channel_id=1, source_target_pairs={{0,1},{1,0},{2,3},{3,2},{4,5},{5,4},{6,7},{7,6},{8,9},{9,8},{10,11... | collective-permute-start | bytes 1966088 | tf_op jit(solution)/shard_map/ppermute | solution.py:207
  135.3 8.2 %collective-permute-start.12 = (bf16[8,64,640]{2,1,0:T(8,128)(2,1)S(1)}, bf16[8,64,640]{2,1,0:T(8,128)(2,1)S(1)}, u32[]{:S(2)}, u32[]{:S(2)}) collective-permute-start(bf16[8,64,640]{2,1,0:T(8,128)(2,1)S(1)} %collective-permute-done.11.rest_2_), channel_id=1, source_target_pairs={{0,1},{1,0},{2,3},{3,2},{4,5},{5,4},{6,7},{7,6},{8,9},{9,8},{10,11... | collective-permute-start | bytes 1966088 | tf_op jit(solution)/shard_map/ppermute | solution.py:207
  135.8 7.7 %collective-permute-start.14 = (bf16[8,64,640]{2,1,0:T(8,128)(2,1)S(1)}, bf16[8,64,640]{2,1,0:T(8,128)(2,1)S(1)}, u32[]{:S(2)}, u32[]{:S(2)}) collective-permute-start(bf16[8,64,640]{2,1,0:T(8,128)(2,1)S(1)} %collective-permute-done.13.rest_4_), channel_id=1, source_target_pairs={{0,1},{1,0},{2,3},{3,2},{4,5},{5,4},{6,7},{7,6},{8,9},{9,8},{10,11... | collective-permute-start | bytes 1966088 | tf_op jit(solution)/shard_map/ppermute | solution.py:207
  135.9 8.5 %collective-permute-start.16 = (bf16[8,64,640]{2,1,0:T(8,128)(2,1)S(1)}, bf16[8,64,640]{2,1,0:T(8,128)(2,1)}, u32[]{:S(2)}, u32[]{:S(2)}) collective-permute-start(bf16[8,64,640]{2,1,0:T(8,128)(2,1)S(1)} %collective-permute-done.15.rest_6_), channel_id=1, source_target_pairs={{0,1},{1,0},{2,3},{3,2},{4,5},{5,4},{6,7},{7,6},{8,9},{9,8},{10,11... | collective-permute-start | bytes 1966088 | tf_op jit(solution)/shard_map/ppermute | solution.py:207
  170.7 10.8 %collective-permute-start.28 = (bf16[4,256,256]{2,1,0:T(8,128)(2,1)S(1)}, bf16[4,256,256]{2,1,0:T(8,128)(2,1)S(1)}, u32[]{:S(2)}, u32[]{:S(2)}) collective-permute-start(bf16[4,256,256]{2,1,0:T(8,128)(2,1)S(1)} %copy-done.12), channel_id=1, source_target_pairs={{0,1},{1,0},{2,3},{3,2},{4,5},{5,4},{6,7},{7,6},{8,9},{9,8},{10,11... | collective-permute-start | bytes 1572872 | tf_op jit(solution)/shard_map/ppermute | solution.py:207
  171.1 8.8 %collective-permute-start.25 = (f32[2,256]{1,0:T(2,128)S(1)}, f32[2,256]{1,0:T(2,128)S(1)}, u32[]{:S(2)}, u32[]{:S(2)}) collective-permute-start(f32[2,256]{1,0:T(2,128)S(1)} %get-tuple-element.46), channel_id=1, source_target_pairs={{0,2},{2,0},{4,6},{6,4},{1,3},{3,1},{5,7},{7,5},{8,10},{10,8},{12,... | collective-permute-start | bytes 6152 | tf_op jit(solution)/shard_map/ppermute | solution.py:207
  171.2 8.8 %collective-permute-start.26 = (f32[2,256]{1,0:T(2,128)S(1)}, f32[2,256]{1,0:T(2,128)S(1)}, u32[]{:S(2)}, u32[]{:S(2)}) collective-permute-start(f32[2,256]{1,0:T(2,128)S(1)} %get-tuple-element.47), channel_id=1, source_target_pairs={{0,4},{2,6},{4,0},{6,2},{1,5},{3,7},{5,1},{7,3},{8,12},{10,14},{12... | collective-permute-start | bytes 6152 | tf_op jit(solution)/shard_map/ppermute | solution.py:207
  178.7 9.2 %collective-permute-start = (bf16[896,256]{1,0:T(8,128)(2,1)}, bf16[896,256]{1,0:T(8,128)(2,1)S(1)}, u32[]{:S(2)}, u32[]{:S(2)}) collective-permute-start(bf16[896,256]{1,0:T(8,128)(2,1)} %bitcast.4), channel_id=1, source_target_pairs={{0,1},{1,0},{2,3},{3,2},{4,5},{5,4},{6,7},{7,6},{8,9},{9,8},{10,11... | collective-permute-start | bytes 1376264 | tf_op jit(solution)/shard_map/ppermute | solution.py:207
  179.9 12.6 %collective-permute-start.1 = (bf16[896,256]{1,0:T(8,128)(2,1)}, bf16[896,256]{1,0:T(8,128)(2,1)}, u32[]{:S(2)}, u32[]{:S(2)}) collective-permute-start(bf16[896,256]{1,0:T(8,128)(2,1)} %bitcast.5), channel_id=1, source_target_pairs={{0,2},{1,3},{2,0},{3,1},{4,6},{5,7},{6,4},{7,5},{8,10},{9,11},{10,... | collective-permute-start | bytes 1376264 | tf_op jit(solution)/shard_map/ppermute | solution.py:207
  184.4 10.8 %collective-permute-start.29 = (bf16[256,256]{1,0:T(8,128)(2,1)S(1)}, bf16[256,256]{1,0:T(8,128)(2,1)S(1)}, u32[]{:S(2)}, u32[]{:S(2)}) collective-permute-start(bf16[256,256]{1,0:T(8,128)(2,1)S(1)} %get-tuple-element.32), channel_id=1, source_target_pairs={{0,2},{2,0},{4,6},{6,4},{1,3},{3,1},{5,7},{7,5},{8,10},{10,8},{12,... | collective-permute-start | bytes 393224 | tf_op jit(solution)/shard_map/ppermute | solution.py:207
  185.8 12.7 %collective-permute-start.30 = (bf16[256,256]{1,0:T(8,128)(2,1)S(1)}, bf16[256,256]{1,0:T(8,128)(2,1)S(1)}, u32[]{:S(2)}, u32[]{:S(2)}) collective-permute-start(bf16[256,256]{1,0:T(8,128)(2,1)S(1)} %get-tuple-element.34), channel_id=1, source_target_pairs={{0,4},{2,6},{4,0},{6,2},{1,5},{3,7},{5,1},{7,3},{8,12},{10,14},{12... | collective-permute-start | bytes 393224 | tf_op jit(solution)/shard_map/ppermute | solution.py:207
  186.4 50.2 %collective-permute-start.2 = (bf16[896,256]{1,0:T(8,128)(2,1)}, bf16[896,256]{1,0:T(8,128)(2,1)S(1)}, u32[]{:S(2)}, u32[]{:S(2)}) collective-permute-start(bf16[896,256]{1,0:T(8,128)(2,1)} %bitcast.6), channel_id=1, source_target_pairs={{0,3},{1,2},{2,1},{3,0},{4,7},{5,6},{6,5},{7,4},{8,11},{9,10},{10,... | collective-permute-start | bytes 1376264 | tf_op jit(solution)/shard_map/ppermute | solution.py:207
  188.0 48.7 %collective-permute-start.3 = (bf16[896,256]{1,0:T(8,128)(2,1)}, bf16[896,256]{1,0:T(8,128)(2,1)}, u32[]{:S(2)}, u32[]{:S(2)}) collective-permute-start(bf16[896,256]{1,0:T(8,128)(2,1)} %bitcast.7), channel_id=1, source_target_pairs={{0,4},{1,5},{2,6},{3,7},{4,0},{5,1},{6,2},{7,3},{8,12},{9,13},{10,... | collective-permute-start | bytes 1376264 | tf_op jit(solution)/shard_map/ppermute | solution.py:207
  192.4 46.6 %collective-permute-start.4 = (bf16[896,256]{1,0:T(8,128)(2,1)}, bf16[896,256]{1,0:T(8,128)(2,1)}, u32[]{:S(2)}, u32[]{:S(2)}) collective-permute-start(bf16[896,256]{1,0:T(8,128)(2,1)} %bitcast.8), channel_id=1, source_target_pairs={{0,5},{1,4},{2,7},{3,6},{4,1},{5,0},{6,3},{7,2},{8,13},{9,12},{10,... | collective-permute-start | bytes 1376264 | tf_op jit(solution)/shard_map/ppermute | solution.py:207
  195.1 45.4 %collective-permute-start.5 = (bf16[896,256]{1,0:T(8,128)(2,1)}, bf16[896,256]{1,0:T(8,128)(2,1)}, u32[]{:S(2)}, u32[]{:S(2)}) collective-permute-start(bf16[896,256]{1,0:T(8,128)(2,1)} %bitcast.9), channel_id=1, source_target_pairs={{0,6},{1,7},{2,4},{3,5},{4,2},{5,3},{6,0},{7,1},{8,14},{9,15},{10,... | collective-permute-start | bytes 1376264 | tf_op jit(solution)/shard_map/ppermute | solution.py:207
  198.5 31.5 %collective-permute-start.31 = (bf16[256,256]{1,0:T(8,128)(2,1)}, bf16[256,256]{1,0:T(8,128)(2,1)}, u32[]{:S(2)}, u32[]{:S(2)}) collective-permute-start(bf16[256,256]{1,0:T(8,128)(2,1)} %get-tuple-element.33), channel_id=1, source_target_pairs={{0,6},{2,4},{4,2},{6,0},{1,7},{3,5},{5,3},{7,1},{8,14},{10,12},{12... | collective-permute-start | bytes 393224 | tf_op jit(solution)/shard_map/ppermute | solution.py:207
  230.0 20.1 %collective-permute-start.6 = (bf16[896,256]{1,0:T(8,128)(2,1)S(1)}, bf16[896,256]{1,0:T(8,128)(2,1)S(1)}, u32[]{:S(2)}, u32[]{:S(2)}) collective-permute-start(bf16[896,256]{1,0:T(8,128)(2,1)S(1)} %bitcast.164), channel_id=1, source_target_pairs={{0,7},{1,6},{2,5},{3,4},{4,3},{5,2},{6,1},{7,0},{8,15},{9,14},{10,... | collective-permute-start | bytes 1376264 | tf_op jit(solution)/shard_map/ppermute | solution.py:207
  236.7 8.4 %collective-permute-start.35 = (bf16[256,256]{1,0:T(8,128)(2,1)S(1)}, bf16[256,256]{1,0:T(8,128)(2,1)S(1)}, u32[]{:S(2)}, u32[]{:S(2)}) collective-permute-start(bf16[256,256]{1,0:T(8,128)(2,1)S(1)} %fusion.3.refs_8_), channel_id=1, source_target_pairs={{0,4},{2,6},{4,0},{6,2},{1,5},{3,7},{5,1},{7,3},{8,12},{10,14},{12... | collective-permute-start | bytes 393224 | tf_op jit(solution)/shard_map/ppermute | solution.py:207
  239.1 11.0 %collective-permute-start.37 = (bf16[256,256]{1,0:T(8,128)(2,1)S(1)}, bf16[256,256]{1,0:T(8,128)(2,1)S(1)}, u32[]{:S(2)}, u32[]{:S(2)}) collective-permute-start(bf16[256,256]{1,0:T(8,128)(2,1)S(1)} %fusion.3.refs_8_), channel_id=1, source_target_pairs={{0,6},{2,4},{4,2},{6,0},{1,7},{3,5},{5,3},{7,1},{8,14},{10,12},{12... | collective-permute-start | bytes 393224 | tf_op jit(solution)/shard_map/ppermute | solution.py:207
  240.5 9.6 %collective-permute-start.32 = (bf16[256,256]{1,0:T(8,128)(2,1)S(1)}, bf16[256,256]{1,0:T(8,128)(2,1)S(1)}, u32[]{:S(2)}, u32[]{:S(2)}) collective-permute-start(bf16[256,256]{1,0:T(8,128)(2,1)S(1)} %fusion.3.refs_8_), channel_id=1, source_target_pairs={{0,1},{1,0},{2,3},{3,2},{4,5},{5,4},{6,7},{7,6},{8,9},{9,8},{10,11... | collective-permute-start | bytes 393224 | tf_op jit(solution)/shard_map/ppermute | solution.py:207
  242.1 8.8 %collective-permute-start.34 = (bf16[256,256]{1,0:T(8,128)(2,1)S(1)}, bf16[256,256]{1,0:T(8,128)(2,1)S(1)}, u32[]{:S(2)}, u32[]{:S(2)}) collective-permute-start(bf16[256,256]{1,0:T(8,128)(2,1)S(1)} %collective-permute-done.33.refs_10_), channel_id=1, source_target_pairs={{0,1},{1,0},{2,3},{3,2},{4,5},{5,4},{6,7},{7,6},{8,9},{9,8},{10,11... | collective-permute-start | bytes 393224 | tf_op jit(solution)/shard_map/ppermute | solution.py:207
  (47 other events, 522.3 us)
Sparse Core Ops, SparseCore 0:
  84.2 41.7 all-gather.1

commit v2 on v1

v2 whole, which is shorter than its diff:
```python
import functools
import math

import jax
import jax.numpy as jnp
from jax import lax
from jax.experimental import pallas as pl
from jax.experimental.pallas import tpu as pltpu
from jax.sharding import Mesh
from jax.sharding import PartitionSpec as P

DR = 64
DN = 128
DV = 128
NEG = -1e30
NZ, NX, NC = 8, 4, 2
NXC = NX * NC
DEV = ("z", "x", "c")
GRP_DEV = ("grp", "z", "x", "c")
XC = ("x", "c")
SMEM = pltpu.SMEM
VMEM = pltpu.VMEM
F32 = jnp.float32
BF16 = jnp.bfloat16
NT = (((1,), (1,)), ((), ()))


def spec(space):
    return pl.BlockSpec(memory_space=space)


SEND, PICK, RANK, VALID, MEMBER, COUNT, SPARE = 0, 4, 8, 16, 24, 32, 40
META = 41
TAIL = 16


def index_kernel(ids, table, lengths, preempted, assignment, meta, *, groups, blocks, block, pages_dev):
    group, column = ids[0], ids[1]
    columns = NZ * NXC
    me = group * columns + column
    place = column & (NXC - 1)
    for i in range(SPARE):
        meta[i] = 0

    def one_request(i, carry):
        slot = preempted[i]
        owner = assignment[i]
        rank = meta[COUNT + owner]
        meta[COUNT + owner] = rank + 1
        ahead = SEND + ((owner - group) & (groups - 1))
        for b in range(blocks):
            page = table[slot, b]
            holder = lax.shift_right_logical(page, pages_dev.bit_length() - 1)
            meta[jnp.where(holder == me, ahead, SPARE)] = page & (pages_dev - 1)

        @pl.when(owner == group)
        def _():
            length = lengths[slot]
            meta[MEMBER + rank] = i
            for b in range(blocks):
                holder = lax.shift_right_logical(table[slot, b], pages_dev.bit_length() - 1)
                col = holder & (columns - 1)
                row = lax.shift_right_logical(holder, columns.bit_length() - 1)
                z = lax.shift_right_logical(col, NXC.bit_length() - 1)
                near = (col & (NXC - 1)) == place
                meta[jnp.where(near, RANK + z, SPARE)] = rank
                meta[jnp.where(near, VALID + z, SPARE)] = jnp.clip(length - b * block, 0, block)
                meta[jnp.where(col == column, PICK, SPARE)] = (group - row) & (groups - 1)

        return carry

    lax.fori_loop(0, preempted.shape[0], one_request, 0)


def pack_kernel(meta, latent, rope, *outs):
    block = latent.shape[1]
    half = rope.shape[1] // 2
    for k, out in enumerate(outs):
        page = meta[SEND + k]
        out[:block, :] = latent[page]
        out[block:, :block] = rope[page, :half, :]
        out[block:, block:] = rope[page, half:, :]


def pick_kernel(meta, *rest):
    sources, out = rest[:-1], rest[-1]
    for k, source in enumerate(sources):

        @pl.when(meta[PICK] == k)
        def _():
            out[0] = source[...]


def rows_kernel(meta, q_nope, q_rope, out, *, q_rows):
    width = q_nope.shape[1]
    for r in range(out.shape[0] // q_rows):
        start = pl.multiple_of(meta[MEMBER + r] * q_rows, q_rows)
        out[r * q_rows : (r + 1) * q_rows, :width] = q_nope[pl.ds(start, q_rows), :]
        out[r * q_rows : (r + 1) * q_rows, width:] = q_rope[pl.ds(start, q_rows), :]


def query_kernel(*refs):
    rows, keys, out = refs[:NXC], refs[NXC:-1], refs[-1]
    per_group = out.shape[0]
    pair = out.shape[1] // NXC
    q_rows = pair // 2
    width = keys[0].shape[0]
    lane = lax.broadcasted_iota(jnp.int32, (rows[0].shape[0], 2 * DR), 1)
    for s in range(NXC):
        hi = rows[s][:, 2 * DN :]
        for h in range(2):
            live = (lane >= h * DR) & (lane < (h + 1) * DR)
            tail = jnp.where(live, hi, jnp.zeros_like(hi))
            lat = lax.dot_general(
                rows[s][:, h * DN : (h + 1) * DN],
                keys[s][:, h * DN : (h + 1) * DN],
                NT,
                preferred_element_type=F32,
            ).astype(BF16)
            lo = s * pair + h * q_rows
            out[:, lo : lo + q_rows, :width] = lat.reshape(per_group, q_rows, width)
            out[:, lo : lo + q_rows, width:] = tail.reshape(per_group, q_rows, 2 * DR)


def three_parts(x):
    high = x.astype(BF16).astype(F32)
    rest = x - high
    middle = rest.astype(BF16).astype(F32)
    return [high, middle, rest - middle]


def stored_stats(stats):
    rows = [p for s in stats for p in three_parts(s)]
    fill = jnp.zeros((TAIL - len(rows), rows[0].shape[1]), F32)
    return jnp.concatenate(rows + [fill], axis=0).astype(BF16)


def read_stats(tail):
    tail = tail.astype(F32)
    return [tail[3 * h : 3 * h + 1] + tail[3 * h + 1 : 3 * h + 2] + tail[3 * h + 2 : 3 * h + 3] for h in range(2)]


def attention_kernel(meta, query, pages_hbm, *rest, scale):
    values = rest[:NXC]
    keep, send, acc, top, total, pages, w_uv, sem, w_sem = rest[NXC:]
    per_group, heads_rows, width = acc.shape
    pair = heads_rows // NXC
    q_rows = pair // 2
    rows = per_group * q_rows
    block = pages.shape[1] * 8 // 9

    loads = [pltpu.make_async_copy(pages_hbm.at[z], pages.at[z], sem.at[z]) for z in range(NZ)]
    loads_w = [
        pltpu.make_async_copy(v.at[:, pl.ds(2 * DN, 2 * DV)], w_uv.at[s], w_sem.at[s])
        for s, v in enumerate(values)
    ]
    for load in loads + loads_w:
        load.start()

    acc[...] = jnp.zeros_like(acc)
    top[...] = jnp.full_like(top, NEG)
    total[...] = jnp.zeros_like(total)

    for z in range(NZ):
        r = meta[RANK + z]
        valid = meta[VALID + z]
        loads[z].wait()

        @pl.when(valid > 0)
        def _():
            latent = pages[z, :block, :]
            tail = pages[z, block:, :]
            rope = jnp.concatenate([tail[:, :block], tail[:, block:]], axis=0)
            rope = jnp.concatenate([rope, rope], axis=0)
            q = query[r]
            score = lax.dot_general(q[:, :width], latent, NT, preferred_element_type=F32)
            score = score + jnp.dot(q[:, width:], rope, preferred_element_type=F32)
            token = lax.broadcasted_iota(jnp.int32, score.shape, 1)
            live = token < valid
            score = jnp.where(live, score * scale, NEG)
            old = top[r][:, :1]
            new = jnp.maximum(old, jnp.max(score, axis=1, keepdims=True))
            expo = jnp.where(live, jnp.exp(score - new), 0.0)
            fade = jnp.exp(old - new)
            top[r] = jnp.broadcast_to(new, top.shape[1:])
            total[r] = total[r] * fade + jnp.sum(expo, axis=1, keepdims=True)
            acc[r] = acc[r] * fade + jnp.dot(
                expo.astype(BF16), latent, preferred_element_type=F32
            )

    for s in range(NXC):
        out = keep if s % 2 == 0 else send
        loads_w[s].wait()
        stats = []
        for h in range(2):
            lo = s * pair + h * q_rows
            weight = total[:, lo : lo + q_rows, :].reshape(rows, total.shape[2])
            high = top[:, lo : lo + q_rows, :].reshape(rows, top.shape[2])
            value = acc[:, lo : lo + q_rows, :].reshape(rows, width)
            some = weight > 0.0
            safe = jnp.where(some, weight, 1.0)
            value = (value / safe[:, :1]).astype(BF16)
            head = jnp.dot(value, w_uv[s, :, h * DV : (h + 1) * DV], preferred_element_type=F32)
            out[s // 2, :rows, h * DV : (h + 1) * DV] = head.astype(BF16)
            stat = jnp.where(some, high + jnp.log(safe), NEG)
            stats.append(stat.T[:1, :])
        out[s // 2, rows:, :] = stored_stats(stats)


def merge(parts, tails):
    rows = parts[0].shape[0]
    stats = [read_stats(t) for t in tails]
    high = [functools.reduce(jnp.maximum, [s[h] for s in stats]) for h in range(2)]
    shares = [[jnp.exp(s[h] - high[h]) for s in stats] for h in range(2)]
    whole = [functools.reduce(jnp.add, shares[h]) for h in range(2)]
    lines = [w / whole[h] for h in range(2) for w in shares[h]]
    fill = jnp.zeros((128 - len(lines), rows), F32)
    table = jnp.concatenate(lines + [fill], axis=0).T
    halves = []
    for h in range(2):
        sides = [p[:, h * DV : (h + 1) * DV].astype(F32) for p in parts]
        first = h * len(parts)
        halves.append(sum(table[:, first + i : first + i + 1] * p for i, p in enumerate(sides)))
    return halves, [high[h] + jnp.log(whole[h]) for h in range(2)]


def chip_kernel(keep, got, *outs):
    for k, out in enumerate(outs):
        rows = out.shape[0] - TAIL
        halves, stats = merge(
            [keep[k, :rows, :], got[k, :rows, :]], [keep[k, rows:, :], got[k, rows:, :]]
        )
        for h, half in enumerate(halves):
            out[:rows, h * DV : (h + 1) * DV] = half.astype(BF16)
        out[rows:, :] = stored_stats(stats)


def heads_kernel(*refs):
    parts, out = refs[:-1], refs[-1]
    rows = out.shape[0]
    halves, _ = merge([p[:rows, :] for p in parts], [p[rows:, :] for p in parts])
    for h, half in enumerate(halves):
        out[:, h * DV : (h + 1) * DV] = half.astype(BF16)


def output_kernel(*refs):
    weights, near, far, out = refs[:NXC], refs[NXC : NXC + NX], refs[-2], refs[-1]
    mixed = None
    for s, w in enumerate(weights):
        heads = near[s // 2][...] if s % 2 == 0 else far[s // 2]
        term = lax.dot_general(w[...], heads, NT, preferred_element_type=F32)
        mixed = term if mixed is None else mixed + term
    out[...] = mixed.astype(BF16)


def sent(x, axis, size, k):
    return lax.ppermute(x, axis, [(i, i ^ k) for i in range(size)])


def gathered(x):
    near = [x] + [sent(x, "x", NX, k) for k in range(1, NX)]
    far = [sent(a, "c", NC, 1) for a in near]
    return [a for pair in zip(near, far) for a in pair]


def local(
    pool_latent,
    pool_rope,
    q_nope,
    q_rope,
    w_uk,
    w_uv,
    w_o,
    block_table,
    lengths,
    preempted,
    assignment,
):
    groups = lax.axis_size("grp")
    group = lax.axis_index("grp")
    column = lax.axis_index(DEV)
    place = lax.axis_index(XC)
    pages_dev, block, width = pool_latent.shape
    requests = preempted.shape[0]
    blocks = block_table.shape[1]
    per_group = requests // groups
    query_rows = q_nope.shape[0] // requests
    rows = per_group * query_rows
    pair = 2 * query_rows
    scale = 1.0 / math.sqrt(DN + DR)
    page_rows = block + DR // 2

    small = pltpu.CompilerParams(vmem_limit_bytes=16 << 20)
    ids = jnp.stack([group, column]).astype(jnp.int32)
    meta = pl.pallas_call(
        functools.partial(
            index_kernel, groups=groups, blocks=blocks, block=block, pages_dev=pages_dev
        ),
        out_shape=jax.ShapeDtypeStruct((META,), jnp.int32),
        in_specs=[spec(SMEM)] * 5,
        out_specs=spec(SMEM),
        name="index",
    )(ids, block_table, lengths, preempted, assignment)

    projections = gathered(jnp.concatenate([w_uk, w_uv], axis=1))

    page_type = jax.ShapeDtypeStruct((page_rows, width), BF16)
    packed = pl.pallas_call(
        pack_kernel,
        out_shape=[page_type] * groups,
        in_specs=[spec(SMEM)] + [spec(VMEM)] * 2,
        out_specs=[spec(VMEM)] * groups,
        compiler_params=small,
        name="pack",
    )(meta, pool_latent, pool_rope)
    arrived = [packed[0]] + [
        lax.ppermute(packed[k], "grp", [(i, (i + k) % groups) for i in range(groups)])
        for k in range(1, groups)
    ]

    own_rows = pl.pallas_call(
        functools.partial(rows_kernel, q_rows=query_rows),
        out_shape=jax.ShapeDtypeStruct((rows, 2 * DN + 2 * DR), BF16),
        in_specs=[spec(SMEM)] + [spec(VMEM)] * 2,
        out_specs=spec(VMEM),
        compiler_params=small,
        name="rows",
    )(meta, q_nope, q_rope)
    all_rows = gathered(own_rows)

    w_cols = w_o.T.reshape(NZ, NXC, w_o.shape[1] // (NZ * NXC), w_o.shape[0])
    pieces = []
    for s in range(NXC):
        part = lax.dynamic_index_in_dim(w_cols, place ^ s, 1, keepdims=False)
        pieces.append(part.reshape(-1, w_o.shape[0]))
    arrived, pieces = lax.optimization_barrier((arrived, pieces))
    weights = [sent(part, XC, NXC, s) if s else part for s, part in enumerate(pieces)]

    own = pl.pallas_call(
        pick_kernel,
        out_shape=jax.ShapeDtypeStruct((1, page_rows, width), BF16),
        in_specs=[spec(SMEM)] + [spec(VMEM)] * groups,
        out_specs=spec(VMEM),
        compiler_params=small,
        name="pick",
    )(meta, *arrived)
    pages = lax.all_gather(own, "z", axis=0, tiled=True)

    query = pl.pallas_call(
        query_kernel,
        out_shape=jax.ShapeDtypeStruct((per_group, NXC * pair, width + 2 * DR), BF16),
        in_specs=[spec(VMEM)] * (2 * NXC),
        out_specs=spec(VMEM),
        compiler_params=small,
        name="query",
    )(*all_rows, *projections)

    pages, weights = lax.optimization_barrier((pages, weights))
    half_type = jax.ShapeDtypeStruct((NX, rows + TAIL, 2 * DV), BF16)
    keep, send = pl.pallas_call(
        functools.partial(attention_kernel, scale=scale),
        out_shape=[half_type, half_type],
        in_specs=[spec(SMEM), spec(VMEM)] + [spec(pl.ANY)] * (1 + NXC),
        out_specs=[spec(VMEM)] * 2,
        scratch_shapes=[
            VMEM((per_group, NXC * pair, width), F32),
            VMEM((per_group, NXC * pair, 128), F32),
            VMEM((per_group, NXC * pair, 128), F32),
            VMEM((NZ, page_rows, width), BF16),
            VMEM((NXC, width, 2 * DV), BF16),
            pltpu.SemaphoreType.DMA((NZ,)),
            pltpu.SemaphoreType.DMA((NXC,)),
        ],
        compiler_params=pltpu.CompilerParams(vmem_limit_bytes=32 << 20),
        name="attention",
    )(meta, query, pages, *projections)

    got = sent(send, "c", NC, 1)
    part_type = jax.ShapeDtypeStruct((rows + TAIL, 2 * DV), BF16)
    chip = pl.pallas_call(
        chip_kernel,
        out_shape=[part_type] * NX,
        in_specs=[spec(VMEM)] * 2,
        out_specs=[spec(VMEM)] * NX,
        compiler_params=small,
        name="chip",
    )(keep, got)
    heads = pl.pallas_call(
        heads_kernel,
        out_shape=jax.ShapeDtypeStruct((rows, 2 * DV), BF16),
        in_specs=[spec(VMEM)] * NX,
        out_specs=spec(VMEM),
        compiler_params=small,
        name="heads",
    )(chip[0], *[sent(chip[k], "x", NX, k) for k in range(1, NX)])
    near = [heads] + [sent(heads, "x", NX, k) for k in range(1, NX)]
    far = sent(jnp.stack(near), "c", NC, 1)

    mixed = pl.pallas_call(
        output_kernel,
        out_shape=jax.ShapeDtypeStruct((weights[0].shape[0], rows), BF16),
        in_specs=[spec(VMEM)] * (NXC + NX + 1),
        out_specs=spec(VMEM),
        compiler_params=small,
        name="output",
    )(*weights, *near, far)
    mixed = lax.all_to_all(mixed, "z", split_axis=0, concat_axis=0, tiled=True)
    mixed = mixed.reshape(NZ, -1, rows).astype(F32).sum(axis=0)
    return mixed.T.astype(BF16)


def solution(mesh):
    split = Mesh(mesh.devices.reshape(mesh.shape["grp"], NZ, NX, NC), GRP_DEV)
    return jax.shard_map(
        local,
        mesh=split,
        in_specs=(
            P(GRP_DEV, None, None),
            P(GRP_DEV, None, None),
            P(None, DEV),
            P(None, DEV),
            P(None, DEV),
            P(None, DEV),
            P(DEV, None),
            P(),
            P(),
            P(),
            P(),
        ),
        out_specs=P("grp", DEV),
        check_vma=False,
    )
```

time: 289 us -> 219 us (0.76)
  Pallas kernels: 77.9 us -> 22.8 us
  waiting for transfers between devices: 97 us -> 85.8 us
    pallas_call x1, Pallas kernels: 37.7 us -> 0.62 us  [local(): pl.pallas_call(pack_kernel, out_shape=[page_type] * groups, in_specs=[spe...]
    ppermute x3, waiting for transfers between devices: 11.9 us -> 1.72 us  [local(): lax.ppermute(packed[k], 'grp', [(i, (i + k) % groups) for i in range(grou...]
    pallas_call x1, Pallas kernels: 10.7 us -> 1.33 us  [local(): pl.pallas_call(pick_kernel, out_shape=jax.ShapeDtypeStruct((1, page_rows,...]
    pallas_call x1, Pallas kernels: 8.51 us -> 3.28 us  [local(): pl.pallas_call(functools.partial(index_kernel, groups=groups, blocks=bloc...]
    broadcast_in_dim x12 -> x0, local copies, waits for them, and re-layouts: 4.01 us -> none  [over_rows(): return jnp.repeat(stat.T, DV, axis=1)]
    unnamed x80 -> x63, local copies, waits for them, and re-layouts: 19 us -> 22.4 us
    pallas_call x1, Pallas kernels: 4.21 us -> 1.15 us  [local(): pl.pallas_call(output_kernel, out_shape=jax.ShapeDtypeStruct((weights[0]....]
    ppermute x36 -> x29, starting transfers between devices: 36.9 us -> 38.1 us  [sent(): return lax.ppermute(x, axis, [(i, i ^ k) for i in range(size)])]
  transfers between devices with their start and end apart: 40 -> 33, of which waited for: 14 -> 22; matrix products, arithmetic and copies ran while one was open for 6% -> 5% of each run, Pallas kernels for 1% -> 1%
where the time goes in v2:
time: 219 us; the launch traced here: 217 us
  waiting for transfers between devices  85.8 us (39%)
  starting transfers between devices  44 us (20%)
  local copies, waits for them, and re-layouts  26.4 us (12%)
  blocking collectives  23.3 us (11%)
  Pallas kernels  22.8 us (10%)
  between operations  13.7 us (6%)
    ppermute x29, waiting for transfers between devices, sent(): return lax.ppermute(x, axis, [(i, i ^ k) for i in range(size)])  84.1 us
    ppermute x29, starting transfers between devices, sent(): return lax.ppermute(x, axis, [(i, i ^ k) for i in range(size)])  38.1 us
    all_to_all x1, blocking collectives, local(): mixed = lax.all_to_all(mixed, 'z', split_axis=0, concat_axis=0, tiled=True)  23.3 us
    unnamed x63, local copies, waits for them, and re-layouts  22.4 us
    pallas_call x1, Pallas kernels, local(): pl.pallas_call(functools.partial(attention_kernel, scale=scale), out_shap...  13.2 us
    ppermute x3, starting transfers between devices, local(): lax.ppermute(packed[k], 'grp', [(i, (i + k) % groups) for i in range(grou...  5.89 us
  transfers between devices with their start and end apart: 33, of which 22 were waited for; matrix products, arithmetic and copies ran while one was open for 5% of the time, Pallas kernels for 1%

profile of v2, /device:TPU:1, one launch (start us, length us, event | category | flops | bytes accessed | tf_op | source)
XLA Modules:
  0.0 217.4 jit_solution(14465440742829475397)
XLA Ops:
  8.6 3.3 %index.1.meta = s32[41]{0:T(128)} custom-call(s32[2]{0:T(128)} %pad_add_fusion.ids, s32[64,8]{1,0:T(8,128)} %copy.23.table, s32[64]{0:T(128)} %lengths.1, s32[32]{0:T(128)} %preempted.1, s32[32]{0:T(128)} %assignment.1), custom_call_target="tpu_custom_call" | custom-call | tf_op jit(solution)/shard_map/index/pallas_call | solution.py:295
  15.0 2.2 %collective-permute-start = (bf16[288,512]{1,0:T(8,128)(2,1)S(1)}, bf16[288,512]{1,0:T(8,128)(2,1)S(1)}, u32[]{:S(2)}, u32[]{:S(2)}) collective-permute-start(bf16[288,512]{1,0:T(8,128)(2,1)S(1)} %get-tuple-element.37), channel_id=1, source_target_pairs={{0,64},{64,128},{128,192},{192,0},{1,65},{65,129},{129,193},{193,1... | collective-permute-start | bytes 884744 | tf_op jit(solution)/shard_map/ppermute | solution.py:317
  17.2 2.6 %collective-permute-start.1 = (bf16[288,512]{1,0:T(8,128)(2,1)S(1)}, bf16[288,512]{1,0:T(8,128)(2,1)S(1)}, u32[]{:S(2)}, u32[]{:S(2)}) collective-permute-start(bf16[288,512]{1,0:T(8,128)(2,1)S(1)} %get-tuple-element.38), channel_id=1, source_target_pairs={{0,128},{64,192},{128,0},{192,64},{1,129},{65,193},{129,1},{193,65... | collective-permute-start | bytes 884744 | tf_op jit(solution)/shard_map/ppermute | solution.py:317
  20.9 5.9 %copy.24 = bf16[256,7168]{0,1:T(8,128)(2,1)} copy(bf16[256,7168]{1,0:T(8,128)(2,1)} %param.17) | data formatting | bytes 7340032 | tf_op args[6]
  26.8 4.0 %constant_dynamic-slice_fusion = (bf16[8,1,112,256]{3,2,1,0:T(8,128)(2,1)}, bf16[8,1,112,256]{3,2,1,0:T(8,128)(2,1)}, bf16[8,1,112,256]{3,2,1,0:T(8,128)(2,1)}, ...) fusion(bf16[8,8,112,256]{3,2,1,0:T(8,128)(2,1)} %bitcast.25, ...), kind=kLoop, calls=%fused_computation.3 | loop fusion | bytes 7340064 | tf_op jit(solution)/shard_map/jit(dynamic_index_in_dim)/dynamic_slice | solution.py:334
  30.8 1.7 collective-permute-done.1.rest_2_
  35.8 2.5 %collective-permute-start.13 = (bf16[256,384]{1,0:T(8,128)(2,1)S(1)}, bf16[256,384]{1,0:T(8,128)(2,1)S(1)}, u32[]{:S(2)}, u32[]{:S(2)}) collective-permute-start(bf16[256,384]{1,0:T(8,128)(2,1)S(1)} %rows.1.refs_0_), channel_id=1, source_target_pairs={{0,4},{2,6},{4,0},{6,2},{1,5},{3,7},{5,1},{7,3},{8,12},{10,14},{12... | collective-permute-start | bytes 589832 | tf_op jit(solution)/shard_map/ppermute | solution.py:257
  38.4 2.4 %collective-permute-start.10 = (bf16[256,384]{1,0:T(8,128)(2,1)S(1)}, bf16[256,384]{1,0:T(8,128)(2,1)S(1)}, u32[]{:S(2)}, u32[]{:S(2)}) collective-permute-start(bf16[256,384]{1,0:T(8,128)(2,1)S(1)} %rows.1.refs_0_), channel_id=1, source_target_pairs={{0,1},{1,0},{2,3},{3,2},{4,5},{5,4},{6,7},{7,6},{8,9},{9,8},{10,11... | collective-permute-start | bytes 589832 | tf_op jit(solution)/shard_map/ppermute | solution.py:257
  40.8 3.1 %collective-permute-start.12 = (bf16[256,384]{1,0:T(8,128)(2,1)S(1)}, bf16[256,384]{1,0:T(8,128)(2,1)S(1)}, u32[]{:S(2)}, u32[]{:S(2)}) collective-permute-start(bf16[256,384]{1,0:T(8,128)(2,1)S(1)} %collective-permute-done.11.refs_2_), channel_id=1, source_target_pairs={{0,1},{1,0},{2,3},{3,2},{4,5},{5,4},{6,7},{7,6},{8,9},{9,8},{10,11... | collective-permute-start | bytes 589832 | tf_op jit(solution)/shard_map/ppermute | solution.py:257
  45.8 1.9 collective-permute-start.20
  49.2 2.1 collective-permute-start.17
  51.4 1.7 collective-permute-done.14.refs_5_
  53.5 4.2 %collective-permute-done.18.refs_10_.rest_2_ = bf16[512,512]{1,0:T(8,128)(2,1)S(1)} collective-permute-done((bf16[512,512]{1,0:T(8,128)(2,1)S(1)}, bf16[512,512]{1,0:T(8,128)(2,1)S(1)}, u32[]{:S(2)}, u32[]{:S(2)}) %collective-permute-start.18) | collective-permute-done | bytes 524320 | tf_op jit(solution)/shard_map/ppermute | solution.py:257
  58.8 12.3 %collective-permute-done.20.refs_12_.rest_4_ = bf16[512,512]{1,0:T(8,128)(2,1)S(1)} collective-permute-done((bf16[512,512]{1,0:T(8,128)(2,1)S(1)}, bf16[512,512]{1,0:T(8,128)(2,1)S(1)}, u32[]{:S(2)}, u32[]{:S(2)}) %collective-permute-start.20) | collective-permute-done | bytes 524320 | tf_op jit(solution)/shard_map/ppermute | solution.py:257
  73.2 2.6 %collective-permute-start.23 = (bf16[512,512]{1,0:T(8,128)(2,1)S(1)}, bf16[512,512]{1,0:T(8,128)(2,1)S(1)}, u32[]{:S(2)}, u32[]{:S(2)}) collective-permute-start(bf16[512,512]{1,0:T(8,128)(2,1)S(1)} %collective-permute-done.22.refs_14_.rest_6_), channel_id=1, source_target_pairs={{0,1},{1,0},{2,3},{3,2},{4,5},{5,4},{6,7},{7,6},{8,9},{9,8},{10,11... | collective-permute-start | bytes 1572872 | tf_op jit(solution)/shard_map/ppermute | solution.py:257
  76.0 2.1 collective-permute-done.3.refs_1_
  78.1 10.0 %collective-permute-done.4.refs_2_ = bf16[896,256]{1,0:T(8,128)(2,1)S(1)} collective-permute-done((bf16[896,256]{1,0:T(8,128)(2,1)}, bf16[896,256]{1,0:T(8,128)(2,1)S(1)}, u32[]{:S(2)}, u32[]{:S(2)}) %collective-permute-start.4) | collective-permute-done | bytes 458784 | tf_op jit(solution)/shard_map/ppermute | solution.py:257
  88.4 4.6 %collective-permute-start.7 = (bf16[896,256]{1,0:T(8,128)(2,1)}, bf16[896,256]{1,0:T(8,128)(2,1)S(1)}, u32[]{:S(2)}, u32[]{:S(2)}) collective-permute-start(bf16[896,256]{1,0:T(8,128)(2,1)} %bitcast.28), channel_id=1, source_target_pairs={{0,5},{1,4},{2,7},{3,6},{4,1},{5,0},{6,3},{7,2},{8,13},{9,12},{10,... | collective-permute-start | bytes 1376264 | tf_op jit(solution)/shard_map/ppermute | solution.py:257
  95.7 2.3 %copy-done = bf16[8,512,640]{2,1,0:T(8,128)(2,1)} copy-done((bf16[8,512,640]{2,1,0:T(8,128)(2,1)}, bf16[8,512,640]{2,1,0:T(8,128)(2,1)S(1)}, u32[]{:S(2)}) %copy-start) | copy-done | bytes 5242904
  100.1 7.7 %collective-permute-done.6.refs_4_ = bf16[896,256]{1,0:T(8,128)(2,1)S(1)} collective-permute-done((bf16[896,256]{1,0:T(8,128)(2,1)}, bf16[896,256]{1,0:T(8,128)(2,1)S(1)}, u32[]{:S(2)}, u32[]{:S(2)}) %collective-permute-start.6) | collective-permute-done | bytes 458784 | tf_op jit(solution)/shard_map/ppermute | solution.py:257
  108.5 9.5 %collective-permute-done.7.refs_5_ = bf16[896,256]{1,0:T(8,128)(2,1)S(1)} collective-permute-done((bf16[896,256]{1,0:T(8,128)(2,1)}, bf16[896,256]{1,0:T(8,128)(2,1)S(1)}, u32[]{:S(2)}, u32[]{:S(2)}) %collective-permute-start.7) | collective-permute-done | bytes 458784 | tf_op jit(solution)/shard_map/ppermute | solution.py:257
  118.8 7.5 %collective-permute-done.8.refs_6_ = bf16[896,256]{1,0:T(8,128)(2,1)S(1)} collective-permute-done((bf16[896,256]{1,0:T(8,128)(2,1)}, bf16[896,256]{1,0:T(8,128)(2,1)S(1)}, u32[]{:S(2)}, u32[]{:S(2)}) %collective-permute-start.8) | collective-permute-done | bytes 458784 | tf_op jit(solution)/shard_map/ppermute | solution.py:257
  127.1 7.3 %collective-permute-done.9.refs_7_ = bf16[896,256]{1,0:T(8,128)(2,1)S(1)} collective-permute-done((bf16[896,256]{1,0:T(8,128)(2,1)}, bf16[896,256]{1,0:T(8,128)(2,1)S(1)}, u32[]{:S(2)}, u32[]{:S(2)}) %collective-permute-start.9) | collective-permute-done | bytes 458784 | tf_op jit(solution)/shard_map/ppermute | solution.py:257
  135.2 2.5 %copy-done.1 = bf16[8,512,640]{2,1,0:T(8,128)(2,1)S(1)} copy-done((bf16[8,512,640]{2,1,0:T(8,128)(2,1)S(1)}, bf16[8,512,640]{2,1,0:T(8,128)(2,1)}, u32[]{:S(2)}) %copy-start.1) | copy-done | bytes 5242904
  141.5 13.2 %attention.1 = (bf16[4,272,256]{2,1,0:T(8,128)(2,1)S(1)}, bf16[4,272,256]{2,1,0:T(8,128)(2,1)S(1)}) custom-call(s32[41]{0:T(128)S(1)} %copy-done.27, bf16[8,512,640]{2,1,0:T(8,128)(2,1)S(1)} %copy-done.1, bf16[8,288,512]{2,1,0:T(8,128)(2,1)S(1)} %copy-done.2, bf16[512,512]{1,0:T(8,128)(2,1)S(1)} %constant_dynamic-update-slice_fusion.refs_8_.rest_0_, ...), custom_call_target="tpu_custom_call" | custom-call | tf_op jit(solution)/shard_map/attention/pallas_call | solution.py:360
  154.7 2.6 %collective-permute-start.24 = (bf16[4,272,256]{2,1,0:T(8,128)(2,1)S(1)}, bf16[4,272,256]{2,1,0:T(8,128)(2,1)S(1)}, u32[]{:S(2)}, u32[]{:S(2)}) collective-permute-start(bf16[4,272,256]{2,1,0:T(8,128)(2,1)S(1)} %get-tuple-element.62), channel_id=1, source_target_pairs={{0,1},{1,0},{2,3},{3,2},{4,5},{5,4},{6,7},{7,6},{8,9},{9,8},{10,11... | collective-permute-start | bytes 1671176 | tf_op jit(solution)/shard_map/ppermute | solution.py:257
  160.0 3.7 %collective-permute-start.27 = (bf16[272,256]{1,0:T(8,128)(2,1)S(1)}, bf16[272,256]{1,0:T(8,128)(2,1)S(1)}, u32[]{:S(2)}, u32[]{:S(2)}) collective-permute-start(bf16[272,256]{1,0:T(8,128)(2,1)S(1)} %get-tuple-element.66), channel_id=1, source_target_pairs={{0,6},{2,4},{4,2},{6,0},{1,7},{3,5},{5,3},{7,1},{8,14},{10,12},{12... | collective-permute-start | bytes 417800 | tf_op jit(solution)/shard_map/ppermute | solution.py:257
  166.4 3.7 %collective-permute-done.27.refs_3_ = bf16[272,256]{1,0:T(8,128)(2,1)S(1)} collective-permute-done((bf16[272,256]{1,0:T(8,128)(2,1)S(1)}, bf16[272,256]{1,0:T(8,128)(2,1)S(1)}, u32[]{:S(2)}, u32[]{:S(2)}) %collective-permute-start.27) | collective-permute-done | bytes 139296 | tf_op jit(solution)/shard_map/ppermute | solution.py:257
  170.7 3.8 %collective-permute-start.29 = (bf16[256,256]{1,0:T(8,128)(2,1)S(1)}, bf16[256,256]{1,0:T(8,128)(2,1)S(1)}, u32[]{:S(2)}, u32[]{:S(2)}) collective-permute-start(bf16[256,256]{1,0:T(8,128)(2,1)S(1)} %heads.1.refs_8_), channel_id=1, source_target_pairs={{0,4},{2,6},{4,0},{6,2},{1,5},{3,7},{5,1},{7,3},{8,12},{10,14},{12... | collective-permute-start | bytes 393224 | tf_op jit(solution)/shard_map/ppermute | solution.py:257
  175.3 4.2 %collective-permute-done.29.refs_10_ = bf16[256,256]{1,0:T(8,128)(2,1)S(1)} collective-permute-done((bf16[256,256]{1,0:T(8,128)(2,1)S(1)}, bf16[256,256]{1,0:T(8,128)(2,1)S(1)}, u32[]{:S(2)}, u32[]{:S(2)}) %collective-permute-start.29) | collective-permute-done | bytes 131104 | tf_op jit(solution)/shard_map/ppermute | solution.py:257
  179.4 2.8 %collective-permute-done.30.refs_11_ = bf16[256,256]{1,0:T(8,128)(2,1)S(1)} collective-permute-done((bf16[256,256]{1,0:T(8,128)(2,1)S(1)}, bf16[256,256]{1,0:T(8,128)(2,1)S(1)}, u32[]{:S(2)}, u32[]{:S(2)}) %collective-permute-start.30) | collective-permute-done | bytes 131104 | tf_op jit(solution)/shard_map/ppermute | solution.py:257
  186.6 23.3 %all_to_all.9 = bf16[8,112,256]{2,1,0:T(8,128)(2,1)S(1)} all-to-all(bf16[8,112,256]{2,1,0:T(8,128)(2,1)S(1)} %bitcast.20), channel_id=1, replica_groups=mesh['grp'=4,'z'=8,'x'=4,'c'=2] {'z'}, dimensions={0} | all-to-all | bytes 917504 | tf_op jit(solution)/shard_map/all_to_all | solution.py:407
  (113 shorter events, 40.4 us)
Async XLA Ops:
  6.5 128.7 %all-gather.2.cloned.1.call-start = ((), (), s32[]{:S(2)}) async-start(), calls=%async_computation.1 | async-start | bytes 2654208 | tf_op jit(solution)/shard_map/all_gather | solution.py:347
  15.0 15.8 %collective-permute-start = (bf16[288,512]{1,0:T(8,128)(2,1)S(1)}, bf16[288,512]{1,0:T(8,128)(2,1)S(1)}, u32[]{:S(2)}, u32[]{:S(2)}) collective-permute-start(bf16[288,512]{1,0:T(8,128)(2,1)S(1)} %get-tuple-element.37), channel_id=1, source_target_pairs={{0,64},{64,128},{128,192},{192,0},{1,65},{65,129},{129,193},{193,1... | collective-permute-start | bytes 884744 | tf_op jit(solution)/shard_map/ppermute | solution.py:317
  17.2 15.4 %collective-permute-start.1 = (bf16[288,512]{1,0:T(8,128)(2,1)S(1)}, bf16[288,512]{1,0:T(8,128)(2,1)S(1)}, u32[]{:S(2)}, u32[]{:S(2)}) collective-permute-start(bf16[288,512]{1,0:T(8,128)(2,1)S(1)} %get-tuple-element.38), channel_id=1, source_target_pairs={{0,128},{64,192},{128,0},{192,64},{1,129},{65,193},{129,1},{193,65... | collective-permute-start | bytes 884744 | tf_op jit(solution)/shard_map/ppermute | solution.py:317
  19.8 12.7 %collective-permute-start.2 = (bf16[288,512]{1,0:T(8,128)(2,1)S(1)}, bf16[288,512]{1,0:T(8,128)(2,1)S(1)}, u32[]{:S(2)}, u32[]{:S(2)}) collective-permute-start(bf16[288,512]{1,0:T(8,128)(2,1)S(1)} %get-tuple-element.39), channel_id=1, source_target_pairs={{0,192},{64,0},{128,64},{192,128},{1,193},{65,1},{129,65},{193,129... | collective-permute-start | bytes 884744 | tf_op jit(solution)/shard_map/ppermute | solution.py:317
  34.5 6.4 %collective-permute-start.11 = (bf16[256,384]{1,0:T(8,128)(2,1)S(1)}, bf16[256,384]{1,0:T(8,128)(2,1)S(1)}, u32[]{:S(2)}, u32[]{:S(2)}) collective-permute-start(bf16[256,384]{1,0:T(8,128)(2,1)S(1)} %rows.1.refs_0_), channel_id=1, source_target_pairs={{0,2},{2,0},{4,6},{6,4},{1,3},{3,1},{5,7},{7,5},{8,10},{10,8},{12,... | collective-permute-start | bytes 589832 | tf_op jit(solution)/shard_map/ppermute | solution.py:257
  35.8 10.0 %collective-permute-start.13 = (bf16[256,384]{1,0:T(8,128)(2,1)S(1)}, bf16[256,384]{1,0:T(8,128)(2,1)S(1)}, u32[]{:S(2)}, u32[]{:S(2)}) collective-permute-start(bf16[256,384]{1,0:T(8,128)(2,1)S(1)} %rows.1.refs_0_), channel_id=1, source_target_pairs={{0,4},{2,6},{4,0},{6,2},{1,5},{3,7},{5,1},{7,3},{8,12},{10,14},{12... | collective-permute-start | bytes 589832 | tf_op jit(solution)/shard_map/ppermute | solution.py:257
  38.2 10.7 %collective-permute-start.15 = (bf16[256,384]{1,0:T(8,128)(2,1)S(1)}, bf16[256,384]{1,0:T(8,128)(2,1)S(1)}, u32[]{:S(2)}, u32[]{:S(2)}) collective-permute-start(bf16[256,384]{1,0:T(8,128)(2,1)S(1)} %rows.1.refs_0_), channel_id=1, source_target_pairs={{0,6},{2,4},{4,2},{6,0},{1,7},{3,5},{5,3},{7,1},{8,14},{10,12},{12... | collective-permute-start | bytes 589832 | tf_op jit(solution)/shard_map/ppermute | solution.py:257
  38.4 10.7 %collective-permute-start.10 = (bf16[256,384]{1,0:T(8,128)(2,1)S(1)}, bf16[256,384]{1,0:T(8,128)(2,1)S(1)}, u32[]{:S(2)}, u32[]{:S(2)}) collective-permute-start(bf16[256,384]{1,0:T(8,128)(2,1)S(1)} %rows.1.refs_0_), channel_id=1, source_target_pairs={{0,1},{1,0},{2,3},{3,2},{4,5},{5,4},{6,7},{7,6},{8,9},{9,8},{10,11... | collective-permute-start | bytes 589832 | tf_op jit(solution)/shard_map/ppermute | solution.py:257
  40.8 10.5 %collective-permute-start.12 = (bf16[256,384]{1,0:T(8,128)(2,1)S(1)}, bf16[256,384]{1,0:T(8,128)(2,1)S(1)}, u32[]{:S(2)}, u32[]{:S(2)}) collective-permute-start(bf16[256,384]{1,0:T(8,128)(2,1)S(1)} %collective-permute-done.11.refs_2_), channel_id=1, source_target_pairs={{0,1},{1,0},{2,3},{3,2},{4,5},{5,4},{6,7},{7,6},{8,9},{9,8},{10,11... | collective-permute-start | bytes 589832 | tf_op jit(solution)/shard_map/ppermute | solution.py:257
  44.0 13.7 %collective-permute-start.18 = (bf16[512,512]{1,0:T(8,128)(2,1)S(1)}, bf16[512,512]{1,0:T(8,128)(2,1)S(1)}, u32[]{:S(2)}, u32[]{:S(2)}) collective-permute-start(bf16[512,512]{1,0:T(8,128)(2,1)S(1)} %constant_dynamic-update-slice_fusion.refs_8_.rest_0_), channel_id=1, source_target_pairs={{0,2},{2,0},{4,6},{6,4},{1,3},{3,1},{5,7},{7,5},{8,10},{10,8},{12,... | collective-permute-start | bytes 1572872 | tf_op jit(solution)/shard_map/ppermute | solution.py:257
  45.8 25.3 %collective-permute-start.20 = (bf16[512,512]{1,0:T(8,128)(2,1)S(1)}, bf16[512,512]{1,0:T(8,128)(2,1)S(1)}, u32[]{:S(2)}, u32[]{:S(2)}) collective-permute-start(bf16[512,512]{1,0:T(8,128)(2,1)S(1)} %constant_dynamic-update-slice_fusion.refs_8_.rest_0_), channel_id=1, source_target_pairs={{0,4},{2,6},{4,0},{6,2},{1,5},{3,7},{5,1},{7,3},{8,12},{10,14},{12... | collective-permute-start | bytes 1572872 | tf_op jit(solution)/shard_map/ppermute | solution.py:257
  49.0 24.2 %collective-permute-start.22 = (bf16[512,512]{1,0:T(8,128)(2,1)S(1)}, bf16[512,512]{1,0:T(8,128)(2,1)S(1)}, u32[]{:S(2)}, u32[]{:S(2)}) collective-permute-start(bf16[512,512]{1,0:T(8,128)(2,1)S(1)} %constant_dynamic-update-slice_fusion.refs_8_.rest_0_), channel_id=1, source_target_pairs={{0,6},{2,4},{4,2},{6,0},{1,7},{3,5},{5,3},{7,1},{8,14},{10,12},{12... | collective-permute-start | bytes 1572872 | tf_op jit(solution)/shard_map/ppermute | solution.py:257
  49.2 26.6 %collective-permute-start.17 = (bf16[512,512]{1,0:T(8,128)(2,1)S(1)}, bf16[512,512]{1,0:T(8,128)(2,1)S(1)}, u32[]{:S(2)}, u32[]{:S(2)}) collective-permute-start(bf16[512,512]{1,0:T(8,128)(2,1)S(1)} %constant_dynamic-update-slice_fusion.refs_8_.rest_0_), channel_id=1, source_target_pairs={{0,1},{1,0},{2,3},{3,2},{4,5},{5,4},{6,7},{7,6},{8,9},{9,8},{10,11... | collective-permute-start | bytes 1572872 | tf_op jit(solution)/shard_map/ppermute | solution.py:257
  53.1 22.6 %collective-permute-start.16 = (bf16[256,384]{1,0:T(8,128)(2,1)S(1)}, bf16[256,384]{1,0:T(8,128)(2,1)S(1)}, u32[]{:S(2)}, u32[]{:S(2)}) collective-permute-start(bf16[256,384]{1,0:T(8,128)(2,1)S(1)} %collective-permute-done.15.refs_6_), channel_id=1, source_target_pairs={{0,1},{1,0},{2,3},{3,2},{4,5},{5,4},{6,7},{7,6},{8,9},{9,8},{10,11... | collective-permute-start | bytes 589832 | tf_op jit(solution)/shard_map/ppermute | solution.py:257
  57.7 30.6 %collective-permute-start.19 = (bf16[512,512]{1,0:T(8,128)(2,1)S(1)}, bf16[512,512]{1,0:T(8,128)(2,1)S(1)}, u32[]{:S(2)}, u32[]{:S(2)}) collective-permute-start(bf16[512,512]{1,0:T(8,128)(2,1)S(1)} %collective-permute-done.18.refs_10_.rest_2_), channel_id=1, source_target_pairs={{0,1},{1,0},{2,3},{3,2},{4,5},{5,4},{6,7},{7,6},{8,9},{9,8},{10,11... | collective-permute-start | bytes 1572872 | tf_op jit(solution)/shard_map/ppermute | solution.py:257
  71.1 21.9 %collective-permute-start.21 = (bf16[512,512]{1,0:T(8,128)(2,1)S(1)}, bf16[512,512]{1,0:T(8,128)(2,1)S(1)}, u32[]{:S(2)}, u32[]{:S(2)}) collective-permute-start(bf16[512,512]{1,0:T(8,128)(2,1)S(1)} %collective-permute-done.20.refs_12_.rest_4_), channel_id=1, source_target_pairs={{0,1},{1,0},{2,3},{3,2},{4,5},{5,4},{6,7},{7,6},{8,9},{9,8},{10,11... | collective-permute-start | bytes 1572872 | tf_op jit(solution)/shard_map/ppermute | solution.py:257
  73.2 20.0 %collective-permute-start.23 = (bf16[512,512]{1,0:T(8,128)(2,1)S(1)}, bf16[512,512]{1,0:T(8,128)(2,1)S(1)}, u32[]{:S(2)}, u32[]{:S(2)}) collective-permute-start(bf16[512,512]{1,0:T(8,128)(2,1)S(1)} %collective-permute-done.22.refs_14_.rest_6_), channel_id=1, source_target_pairs={{0,1},{1,0},{2,3},{3,2},{4,5},{5,4},{6,7},{7,6},{8,9},{9,8},{10,11... | collective-permute-start | bytes 1572872 | tf_op jit(solution)/shard_map/ppermute | solution.py:257
  75.7 2.4 %collective-permute-start.3 = (bf16[896,256]{1,0:T(8,128)(2,1)}, bf16[896,256]{1,0:T(8,128)(2,1)S(1)}, u32[]{:S(2)}, u32[]{:S(2)}) collective-permute-start(bf16[896,256]{1,0:T(8,128)(2,1)} %bitcast.32), channel_id=1, source_target_pairs={{0,1},{1,0},{2,3},{3,2},{4,5},{5,4},{6,7},{7,6},{8,9},{9,8},{10,11... | collective-permute-start | bytes 1376264 | tf_op jit(solution)/shard_map/ppermute | solution.py:257
  75.7 12.4 %collective-permute-start.4 = (bf16[896,256]{1,0:T(8,128)(2,1)}, bf16[896,256]{1,0:T(8,128)(2,1)S(1)}, u32[]{:S(2)}, u32[]{:S(2)}) collective-permute-start(bf16[896,256]{1,0:T(8,128)(2,1)} %bitcast.31), channel_id=1, source_target_pairs={{0,2},{1,3},{2,0},{3,1},{4,6},{5,7},{6,4},{7,5},{8,10},{9,11},{10,... | collective-permute-start | bytes 1376264 | tf_op jit(solution)/shard_map/ppermute | solution.py:257
  78.1 21.1 %collective-permute-start.5 = (bf16[896,256]{1,0:T(8,128)(2,1)}, bf16[896,256]{1,0:T(8,128)(2,1)S(1)}, u32[]{:S(2)}, u32[]{:S(2)}) collective-permute-start(bf16[896,256]{1,0:T(8,128)(2,1)} %bitcast.30), channel_id=1, source_target_pairs={{0,3},{1,2},{2,1},{3,0},{4,7},{5,6},{6,5},{7,4},{8,11},{9,10},{10,... | collective-permute-start | bytes 1376264 | tf_op jit(solution)/shard_map/ppermute | solution.py:257
  88.1 19.6 %collective-permute-start.6 = (bf16[896,256]{1,0:T(8,128)(2,1)}, bf16[896,256]{1,0:T(8,128)(2,1)S(1)}, u32[]{:S(2)}, u32[]{:S(2)}) collective-permute-start(bf16[896,256]{1,0:T(8,128)(2,1)} %bitcast.29), channel_id=1, source_target_pairs={{0,4},{1,5},{2,6},{3,7},{4,0},{5,1},{6,2},{7,3},{8,12},{9,13},{10,... | collective-permute-start | bytes 1376264 | tf_op jit(solution)/shard_map/ppermute | solution.py:257
  88.4 29.6 %collective-permute-start.7 = (bf16[896,256]{1,0:T(8,128)(2,1)}, bf16[896,256]{1,0:T(8,128)(2,1)S(1)}, u32[]{:S(2)}, u32[]{:S(2)}) collective-permute-start(bf16[896,256]{1,0:T(8,128)(2,1)} %bitcast.28), channel_id=1, source_target_pairs={{0,5},{1,4},{2,7},{3,6},{4,1},{5,0},{6,3},{7,2},{8,13},{9,12},{10,... | collective-permute-start | bytes 1376264 | tf_op jit(solution)/shard_map/ppermute | solution.py:257
  93.0 33.3 %collective-permute-start.8 = (bf16[896,256]{1,0:T(8,128)(2,1)}, bf16[896,256]{1,0:T(8,128)(2,1)S(1)}, u32[]{:S(2)}, u32[]{:S(2)}) collective-permute-start(bf16[896,256]{1,0:T(8,128)(2,1)} %bitcast.27), channel_id=1, source_target_pairs={{0,6},{1,7},{2,4},{3,5},{4,2},{5,3},{6,0},{7,1},{8,14},{9,15},{10,... | collective-permute-start | bytes 1376264 | tf_op jit(solution)/shard_map/ppermute | solution.py:257
  93.2 41.2 %collective-permute-start.9 = (bf16[896,256]{1,0:T(8,128)(2,1)}, bf16[896,256]{1,0:T(8,128)(2,1)S(1)}, u32[]{:S(2)}, u32[]{:S(2)}) collective-permute-start(bf16[896,256]{1,0:T(8,128)(2,1)} %bitcast.26), channel_id=1, source_target_pairs={{0,7},{1,6},{2,5},{3,4},{4,3},{5,2},{6,1},{7,0},{8,15},{9,14},{10,... | collective-permute-start | bytes 1376264 | tf_op jit(solution)/shard_map/ppermute | solution.py:257
  154.7 4.2 %collective-permute-start.24 = (bf16[4,272,256]{2,1,0:T(8,128)(2,1)S(1)}, bf16[4,272,256]{2,1,0:T(8,128)(2,1)S(1)}, u32[]{:S(2)}, u32[]{:S(2)}) collective-permute-start(bf16[4,272,256]{2,1,0:T(8,128)(2,1)S(1)} %get-tuple-element.62), channel_id=1, source_target_pairs={{0,1},{1,0},{2,3},{3,2},{4,5},{5,4},{6,7},{7,6},{8,9},{9,8},{10,11... | collective-permute-start | bytes 1671176 | tf_op jit(solution)/shard_map/ppermute | solution.py:257
  159.8 5.0 %collective-permute-start.25 = (bf16[272,256]{1,0:T(8,128)(2,1)S(1)}, bf16[272,256]{1,0:T(8,128)(2,1)S(1)}, u32[]{:S(2)}, u32[]{:S(2)}) collective-permute-start(bf16[272,256]{1,0:T(8,128)(2,1)S(1)} %get-tuple-element.64), channel_id=1, source_target_pairs={{0,2},{2,0},{4,6},{6,4},{1,3},{3,1},{5,7},{7,5},{8,10},{10,8},{12,... | collective-permute-start | bytes 417800 | tf_op jit(solution)/shard_map/ppermute | solution.py:257
  159.9 6.5 %collective-permute-start.26 = (bf16[272,256]{1,0:T(8,128)(2,1)S(1)}, bf16[272,256]{1,0:T(8,128)(2,1)S(1)}, u32[]{:S(2)}, u32[]{:S(2)}) collective-permute-start(bf16[272,256]{1,0:T(8,128)(2,1)S(1)} %get-tuple-element.65), channel_id=1, source_target_pairs={{0,4},{2,6},{4,0},{6,2},{1,5},{3,7},{5,1},{7,3},{8,12},{10,14},{12... | collective-permute-start | bytes 417800 | tf_op jit(solution)/shard_map/ppermute | solution.py:257
  160.0 10.1 %collective-permute-start.27 = (bf16[272,256]{1,0:T(8,128)(2,1)S(1)}, bf16[272,256]{1,0:T(8,128)(2,1)S(1)}, u32[]{:S(2)}, u32[]{:S(2)}) collective-permute-start(bf16[272,256]{1,0:T(8,128)(2,1)S(1)} %get-tuple-element.66), channel_id=1, source_target_pairs={{0,6},{2,4},{4,2},{6,0},{1,7},{3,5},{5,3},{7,1},{8,14},{10,12},{12... | collective-permute-start | bytes 417800 | tf_op jit(solution)/shard_map/ppermute | solution.py:257
  170.6 4.7 %collective-permute-start.28 = (bf16[256,256]{1,0:T(8,128)(2,1)S(1)}, bf16[256,256]{1,0:T(8,128)(2,1)S(1)}, u32[]{:S(2)}, u32[]{:S(2)}) collective-permute-start(bf16[256,256]{1,0:T(8,128)(2,1)S(1)} %heads.1.refs_8_), channel_id=1, source_target_pairs={{0,2},{2,0},{4,6},{6,4},{1,3},{3,1},{5,7},{7,5},{8,10},{10,8},{12,... | collective-permute-start | bytes 393224 | tf_op jit(solution)/shard_map/ppermute | solution.py:257
  170.7 8.7 %collective-permute-start.29 = (bf16[256,256]{1,0:T(8,128)(2,1)S(1)}, bf16[256,256]{1,0:T(8,128)(2,1)S(1)}, u32[]{:S(2)}, u32[]{:S(2)}) collective-permute-start(bf16[256,256]{1,0:T(8,128)(2,1)S(1)} %heads.1.refs_8_), channel_id=1, source_target_pairs={{0,4},{2,6},{4,0},{6,2},{1,5},{3,7},{5,1},{7,3},{8,12},{10,14},{12... | collective-permute-start | bytes 393224 | tf_op jit(solution)/shard_map/ppermute | solution.py:257
  174.5 7.7 %collective-permute-start.30 = (bf16[256,256]{1,0:T(8,128)(2,1)S(1)}, bf16[256,256]{1,0:T(8,128)(2,1)S(1)}, u32[]{:S(2)}, u32[]{:S(2)}) collective-permute-start(bf16[256,256]{1,0:T(8,128)(2,1)S(1)} %heads.1.refs_8_), channel_id=1, source_target_pairs={{0,6},{2,4},{4,2},{6,0},{1,7},{3,5},{5,3},{7,1},{8,14},{10,12},{12... | collective-permute-start | bytes 393224 | tf_op jit(solution)/shard_map/ppermute | solution.py:257
  182.3 3.1 %collective-permute-start.31 = (bf16[4,256,256]{2,1,0:T(8,128)(2,1)S(1)}, bf16[4,256,256]{2,1,0:T(8,128)(2,1)S(1)}, u32[]{:S(2)}, u32[]{:S(2)}) collective-permute-start(bf16[4,256,256]{2,1,0:T(8,128)(2,1)S(1)} %pad_maximum_fusion), channel_id=1, source_target_pairs={{0,1},{1,0},{2,3},{3,2},{4,5},{5,4},{6,7},{7,6},{8,9},{9,8},{10,11... | collective-permute-start | bytes 1572872 | tf_op jit(solution)/shard_map/ppermute | solution.py:257
  (31 other events, 449.6 us)
Sparse Core Ops, SparseCore 0:
  34.0 41.8 all-gather.1

commit v3 on v2

--- a/solution.py
+++ b/solution.py
@@ -29,18 +29,21 @@
     return pl.BlockSpec(memory_space=space)
 
 
-SEND, PICK, RANK, VALID, MEMBER, COUNT, SPARE = 0, 4, 8, 16, 24, 32, 40
+SEND, PICK, PLACE, RANK, VALID, MEMBER, COUNT, SPARE = 0, 4, 5, 8, 16, 24, 32, 40
 META = 41
 TAIL = 16
 
 
-def index_kernel(ids, table, lengths, preempted, assignment, meta, *, groups, blocks, block, pages_dev):
+def fill_table(meta, ids, table, lengths, preempted, assignment, *, groups, block, pages_dev):
     group, column = ids[0], ids[1]
+    blocks = table.shape[0]
     columns = NZ * NXC
     me = group * columns + column
     place = column & (NXC - 1)
+    plane = lax.shift_right_logical(column, NXC.bit_length() - 1)
     for i in range(SPARE):
         meta[i] = 0
+    meta[PLACE] = place
 
     def one_request(i, carry):
         slot = preempted[i]
@@ -49,7 +52,7 @@
         meta[COUNT + owner] = rank + 1
         ahead = SEND + ((owner - group) & (groups - 1))
         for b in range(blocks):
-            page = table[slot, b]
+            page = table[b, slot]
             holder = lax.shift_right_logical(page, pages_dev.bit_length() - 1)
             meta[jnp.where(holder == me, ahead, SPARE)] = page & (pages_dev - 1)
 
@@ -58,10 +61,10 @@
             length = lengths[slot]
             meta[MEMBER + rank] = i
             for b in range(blocks):
-                holder = lax.shift_right_logical(table[slot, b], pages_dev.bit_length() - 1)
+                holder = lax.shift_right_logical(table[b, slot], pages_dev.bit_length() - 1)
                 col = holder & (columns - 1)
                 row = lax.shift_right_logical(holder, columns.bit_length() - 1)
-                z = lax.shift_right_logical(col, NXC.bit_length() - 1)
+                z = (lax.shift_right_logical(col, NXC.bit_length() - 1) - plane) & (NZ - 1)
                 near = (col & (NXC - 1)) == place
                 meta[jnp.where(near, RANK + z, SPARE)] = rank
                 meta[jnp.where(near, VALID + z, SPARE)] = jnp.clip(length - b * block, 0, block)
@@ -72,14 +75,54 @@
     lax.fori_loop(0, preempted.shape[0], one_request, 0)
 
 
-def pack_kernel(meta, latent, rope, *outs):
-    block = latent.shape[1]
+def prepare_kernel(ids, *refs, groups):
+    tables_hbm, (latent_hbm, rope_hbm, q_nope, q_rope), rest = refs[:4], refs[4:8], refs[8:]
+    meta, own_rows = rest[:2]
+    outs = rest[2 : 2 + groups]
+    table, lengths, preempted, assignment, latent, rope, sem, row_sem, table_sem = rest[2 + groups :]
+    tables = (table, lengths, preempted, assignment)
+    pages_dev, block, _ = latent.shape
     half = rope.shape[1] // 2
+    q_rows = q_nope.shape[0] // preempted.shape[0]
+    width = q_nope.shape[1]
+    loads = [
+        pltpu.make_async_copy(latent_hbm, latent, sem.at[0]),
+        pltpu.make_async_copy(rope_hbm, rope, sem.at[1]),
+    ]
+    first = [
+        pltpu.make_async_copy(src, dst, table_sem.at[i])
+        for i, (src, dst) in enumerate(zip(tables_hbm, tables))
+    ]
+    for load in first + loads:
+        load.start()
+    for load in first:
+        load.wait()
+    fill_table(
+        meta, ids, table, lengths, preempted, assignment,
+        groups=groups, block=block, pages_dev=pages_dev,
+    )
+    moves = []
+    for r in range(own_rows.shape[0] // q_rows):
+        start = pl.multiple_of(meta[MEMBER + r] * q_rows, q_rows)
+        for j, (source, lo, hi) in enumerate(((q_nope, 0, width), (q_rope, width, own_rows.shape[1]))):
+            moves.append(
+                pltpu.make_async_copy(
+                    source.at[pl.ds(start, q_rows), :],
+                    own_rows.at[pl.ds(r * q_rows, q_rows), pl.ds(lo, hi - lo)],
+                    row_sem.at[r, j],
+                )
+            )
+    for move in moves:
+        move.start()
+    for load in loads:
+        load.wait()
     for k, out in enumerate(outs):
         page = meta[SEND + k]
         out[:block, :] = latent[page]
         out[block:, :block] = rope[page, :half, :]
         out[block:, block:] = rope[page, half:, :]
+    for move in moves:
+        move.wait()
 
 
 def pick_kernel(meta, *rest):
@@ -88,32 +131,34 @@
 
         @pl.when(meta[PICK] == k)
         def _():
-            out[0] = source[...]
-
-
-def rows_kernel(meta, q_nope, q_rope, out, *, q_rows):
-    width = q_nope.shape[1]
-    for r in range(out.shape[0] // q_rows):
-        start = pl.multiple_of(meta[MEMBER + r] * q_rows, q_rows)
-        out[r * q_rows : (r + 1) * q_rows, :width] = q_nope[pl.ds(start, q_rows), :]
-        out[r * q_rows : (r + 1) * q_rows, width:] = q_rope[pl.ds(start, q_rows), :]
-
-
-def query_kernel(*refs):
-    rows, keys, out = refs[:NXC], refs[NXC:-1], refs[-1]
+            out[...] = source[...]
+
+
+def query_kernel(meta, *refs):
+    near, far, keys_hbm, out, keys, sem = refs[:NX], *refs[NX:]
     per_group = out.shape[0]
     pair = out.shape[1] // NXC
     q_rows = pair // 2
-    width = keys[0].shape[0]
-    lane = lax.broadcasted_iota(jnp.int32, (rows[0].shape[0], 2 * DR), 1)
+    width = keys.shape[1]
+    loads = [
+        pltpu.make_async_copy(
+            keys_hbm.at[meta[PLACE] ^ s, :, pl.ds(0, 2 * DN)], keys.at[s], sem.at[s]
+        )
+        for s in range(NXC)
+    ]
+    for load in loads:
+        load.start()
+    lane = lax.broadcasted_iota(jnp.int32, (near[0].shape[0], 2 * DR), 1)
     for s in range(NXC):
-        hi = rows[s][:, 2 * DN :]
+        rows = near[s // 2] if s % 2 == 0 else far.at[s // 2]
+        loads[s].wait()
+        hi = rows[:, 2 * DN :]
         for h in range(2):
             live = (lane >= h * DR) & (lane < (h + 1) * DR)
             tail = jnp.where(live, hi, jnp.zeros_like(hi))
             lat = lax.dot_general(
-                rows[s][:, h * DN : (h + 1) * DN],
-                keys[s][:, h * DN : (h + 1) * DN],
+                rows[:, h * DN : (h + 1) * DN],
+                keys[s, :, h * DN : (h + 1) * DN],
                 NT,
                 preferred_element_type=F32,
             ).astype(BF16)
@@ -140,31 +185,43 @@
     return [tail[3 * h : 3 * h + 1] + tail[3 * h + 1 : 3 * h + 2] + tail[3 * h + 2 : 3 * h + 3] for h in range(2)]
 
 
-def attention_kernel(meta, query, pages_hbm, *rest, scale):
-    values = rest[:NXC]
-    keep, send, acc, top, total, pages, w_uv, sem, w_sem = rest[NXC:]
+def attention_kernel(meta, query, values, *rest, scale):
+    sources = rest[: NZ + 1]
+    keep, send, acc, top, total, pages, w_uv, sem, w_sem = rest[NZ + 1 :]
     per_group, heads_rows, width = acc.shape
     pair = heads_rows // NXC
     q_rows = pair // 2
     rows = per_group * q_rows
     block = pages.shape[1] * 8 // 9
 
-    loads = [pltpu.make_async_copy(pages_hbm.at[z], pages.at[z], sem.at[z]) for z in range(NZ)]
+    middle = NZ // 2
+    split = pages.shape[1] // 2
+    loads = {
+        z: [pltpu.make_async_copy(sources[z], pages.at[z], sem.at[z])] for z in range(NZ) if z != middle
+    }
+    loads[middle] = [
+        pltpu.make_async_copy(sources[middle], pages.at[middle, pl.ds(0, split), :], sem.at[middle]),
+        pltpu.make_async_copy(sources[NZ], pages.at[middle, pl.ds(split, split), :], sem.at[NZ]),
+    ]
+    order = [0] + [z for k in range(1, middle) for z in (k, NZ - k)] + [middle]
     loads_w = [
-        pltpu.make_async_copy(v.at[:, pl.ds(2 * DN, 2 * DV)], w_uv.at[s], w_sem.at[s])
-        for s, v in enumerate(values)
-    ]
-    for load in loads + loads_w:
+        pltpu.make_async_copy(
+            values.at[meta[PLACE] ^ s, :, pl.ds(2 * DN, 2 * DV)], w_uv.at[s], w_sem.at[s]
+        )
+        for s in range(NXC)
+    ]
+    for load in [c for z in order for c in loads[z]] + loads_w:
         load.start()
 
     acc[...] = jnp.zeros_like(acc)
     top[...] = jnp.full_like(top, NEG)
     total[...] = jnp.zeros_like(total)
 
-    for z in range(NZ):
+    for z in order:
         r = meta[RANK + z]
         valid = meta[VALID + z]
-        loads[z].wait()
+        for load in loads[z]:
+            load.wait()
 
         @pl.when(valid > 0)
         def _():
@@ -199,7 +256,7 @@
             value = acc[:, lo : lo + q_rows, :].reshape(rows, width)
             some = weight > 0.0
             safe = jnp.where(some, weight, 1.0)
-            value = (value / safe[:, :1]).astype(BF16)
+            value = (value * (1.0 / safe)[:, :1]).astype(BF16)
             head = jnp.dot(value, w_uv[s, :, h * DV : (h + 1) * DV], preferred_element_type=F32)
             out[s // 2, :rows, h * DV : (h + 1) * DV] = head.astype(BF16)
             stat = jnp.where(some, high + jnp.log(safe), NEG)
@@ -243,14 +300,24 @@
         out[:, h * DV : (h + 1) * DV] = half.astype(BF16)
 
 
-def output_kernel(*refs):
-    weights, near, far, out = refs[:NXC], refs[NXC : NXC + NX], refs[-2], refs[-1]
-    mixed = None
-    for s, w in enumerate(weights):
-        heads = near[s // 2][...] if s % 2 == 0 else far[s // 2]
-        term = lax.dot_general(w[...], heads, NT, preferred_element_type=F32)
-        mixed = term if mixed is None else mixed + term
-    out[...] = mixed.astype(BF16)
+def output_kernel(weights, *refs):
+    near, far, out = refs[:NX], refs[-2], refs[-1]
+    share = weights.shape[3]
+    for y in range(weights.shape[0]):
+        mixed = None
+        for s in range(NXC):
+            heads = near[s // 2][...] if s % 2 == 0 else far[s // 2]
+            term = lax.dot_general(weights[y, s % 2, s // 2], heads, NT, preferred_element_type=F32)
+            mixed = term if mixed is None else mixed + term
+        out[y * share : (y + 1) * share, :] = mixed.astype(BF16)
+
+
+def after(x, *others):
+    return lax.optimization_barrier((x, *others))[0]
+
+
+def in_hbm(x):
+    return pltpu.with_memory_space_constraint(x, pltpu.HBM)
 
 
 def sent(x, axis, size, k):
@@ -259,8 +326,11 @@
 
 def gathered(x):
     near = [x] + [sent(x, "x", NX, k) for k in range(1, NX)]
-    far = [sent(a, "c", NC, 1) for a in near]
-    return [a for pair in zip(near, far) for a in pair]
+    return near, sent(jnp.stack(near), "c", NC, 1)
+
+
+def shifted(x, k):
+    return lax.ppermute(x, "z", [(i, (i + k) % NZ) for i in range(NZ)])
 
 
 def local(
@@ -291,76 +361,94 @@
     page_rows = block + DR // 2
 
     small = pltpu.CompilerParams(vmem_limit_bytes=16 << 20)
+    projections = in_hbm(lax.all_gather(jnp.concatenate([w_uk, w_uv], axis=1), XC, axis=0))
+
     ids = jnp.stack([group, column]).astype(jnp.int32)
-    meta = pl.pallas_call(
-        functools.partial(
-            index_kernel, groups=groups, blocks=blocks, block=block, pages_dev=pages_dev
-        ),
-        out_shape=jax.ShapeDtypeStruct((META,), jnp.int32),
-        in_specs=[spec(SMEM)] * 5,
-        out_specs=spec(SMEM),
-        name="index",
-    )(ids, block_table, lengths, preempted, assignment)
-
-    projections = gathered(jnp.concatenate([w_uk, w_uv], axis=1))
-
     page_type = jax.ShapeDtypeStruct((page_rows, width), BF16)
-    packed = pl.pallas_call(
-        pack_kernel,
-        out_shape=[page_type] * groups,
-        in_specs=[spec(SMEM)] + [spec(VMEM)] * 2,
-        out_specs=[spec(VMEM)] * groups,
+    meta, own_rows, *packed = pl.pallas_call(
+        functools.partial(prepare_kernel, groups=groups),
+        out_shape=[
+            jax.ShapeDtypeStruct((META,), jnp.int32),
+            jax.ShapeDtypeStruct((rows, 2 * DN + 2 * DR), BF16),
+        ]
+        + [page_type] * groups,
+        in_specs=[spec(SMEM)] + [spec(pltpu.HBM)] * 8,
+        out_specs=[spec(SMEM)] + [spec(VMEM)] * (1 + groups),
+        scratch_shapes=[
+            SMEM(block_table.T.shape, jnp.int32),
+            SMEM(lengths.shape, jnp.int32),
+            SMEM(preempted.shape, jnp.int32),
+            SMEM(assignment.shape, jnp.int32),
+            VMEM(pool_latent.shape, BF16),
+            VMEM(pool_rope.shape, BF16),
+            pltpu.SemaphoreType.DMA((2,)),
+            pltpu.SemaphoreType.DMA((per_group, 2)),
+            pltpu.SemaphoreType.DMA((4,)),
+        ],
         compiler_params=small,
-        name="pack",
-    )(meta, pool_latent, pool_rope)
+        name="prepare",
+    )(ids, *[in_hbm(a) for a in (block_table.T, lengths, preempted, assignment, pool_latent, pool_rope, q_nope, q_rope)])
+
     arrived = [packed[0]] + [
         lax.ppermute(packed[k], "grp", [(i, (i + k) % groups) for i in range(groups)])
         for k in range(1, groups)
     ]
-
-    own_rows = pl.pallas_call(
-        functools.partial(rows_kernel, q_rows=query_rows),
-        out_shape=jax.ShapeDtypeStruct((rows, 2 * DN + 2 * DR), BF16),
-        in_specs=[spec(SMEM)] + [spec(VMEM)] * 2,
-        out_specs=spec(VMEM),
-        compiler_params=small,
-        name="rows",
-    )(meta, q_nope, q_rope)
-    all_rows = gathered(own_rows)
-
-    w_cols = w_o.T.reshape(NZ, NXC, w_o.shape[1] // (NZ * NXC), w_o.shape[0])
-    pieces = []
-    for s in range(NXC):
-        part = lax.dynamic_index_in_dim(w_cols, place ^ s, 1, keepdims=False)
-        pieces.append(part.reshape(-1, w_o.shape[0]))
-    arrived, pieces = lax.optimization_barrier((arrived, pieces))
-    weights = [sent(part, XC, NXC, s) if s else part for s, part in enumerate(pieces)]
+    near_rows = [own_rows] + [sent(own_rows, "x", NX, k) for k in range(1, NX)]
+
+    share = w_o.shape[1] // groups
+    planes = NZ // groups
+    w_part = lax.dynamic_slice_in_dim(w_o, group * share, share, 1)
+    w_cols = w_part.T.reshape(planes, NX, NC, share // (planes * NXC), w_o.shape[0])
+    pieces = [
+        lax.dynamic_index_in_dim(w_cols, (place // NC) ^ k, 1, keepdims=False) for k in range(NX)
+    ]
+    arrived, near_rows, pieces = lax.optimization_barrier((arrived, near_rows, pieces))
 
     own = pl.pallas_call(
         pick_kernel,
-        out_shape=jax.ShapeDtypeStruct((1, page_rows, width), BF16),
+        out_shape=page_type,
         in_specs=[spec(SMEM)] + [spec(VMEM)] * groups,
         out_specs=spec(VMEM),
         compiler_params=small,
         name="pick",
     )(meta, *arrived)
-    pages = lax.all_gather(own, "z", axis=0, tiled=True)
+
+    far_rows = sent(jnp.stack(near_rows), "c", NC, 1)
+    own, pieces = lax.optimization_barrier((own, pieces))
+    below, above = [own], [own]
+    for k in range(1, NZ // 2):
+        below.append(shifted(below[-1], 1))
+        above.append(shifted(above[-1], -1))
+    low = shifted(below[-1][: page_rows // 2], 1)
+    high = shifted(above[-1][page_rows // 2 :], -1)
+    pages = [own] + above[1:] + [low] + below[:0:-1] + [high]
+
+    columns = jnp.stack([sent(part, "x", NX, k) if k else part for k, part in enumerate(pieces)])
+    columns = after(columns, above[2], below[2])
+    core = place % NC
+    mine = lax.dynamic_index_in_dim(columns, core, 2, keepdims=False)
+    theirs = sent(lax.dynamic_index_in_dim(columns, 1 - core, 2, keepdims=False), "c", NC, 1)
+    quarter = jnp.stack([mine, theirs]).reshape(NC, NX, share // NXC, w_o.shape[0])
+    weights = lax.all_gather(after(quarter, above[3], below[3]), "grp", axis=0)
 
     query = pl.pallas_call(
         query_kernel,
         out_shape=jax.ShapeDtypeStruct((per_group, NXC * pair, width + 2 * DR), BF16),
-        in_specs=[spec(VMEM)] * (2 * NXC),
+        in_specs=[spec(SMEM)] + [spec(VMEM)] * (NX + 1) + [spec(pltpu.HBM)],
         out_specs=spec(VMEM),
+        scratch_shapes=[
+            VMEM((NXC, width, 2 * DN), BF16),
+            pltpu.SemaphoreType.DMA((NXC,)),
+        ],
         compiler_params=small,
         name="query",
-    )(*all_rows, *projections)
-
-    pages, weights = lax.optimization_barrier((pages, weights))
+    )(meta, *near_rows, far_rows, projections)
+
     half_type = jax.ShapeDtypeStruct((NX, rows + TAIL, 2 * DV), BF16)
     keep, send = pl.pallas_call(
         functools.partial(attention_kernel, scale=scale),
         out_shape=[half_type, half_type],
-        in_specs=[spec(SMEM), spec(VMEM)] + [spec(pl.ANY)] * (1 + NXC),
+        in_specs=[spec(SMEM), spec(VMEM), spec(pltpu.HBM)] + [spec(pl.ANY)] * (1 + NZ),
         out_specs=[spec(VMEM)] * 2,
         scratch_shapes=[
             VMEM((per_group, NXC * pair, width), F32),
@@ -368,12 +456,12 @@
             VMEM((per_group, NXC * pair, 128), F32),
             VMEM((NZ, page_rows, width), BF16),
             VMEM((NXC, width, 2 * DV), BF16),
-            pltpu.SemaphoreType.DMA((NZ,)),
+            pltpu.SemaphoreType.DMA((NZ + 1,)),
             pltpu.SemaphoreType.DMA((NXC,)),
         ],
         compiler_params=pltpu.CompilerParams(vmem_limit_bytes=32 << 20),
         name="attention",
-    )(meta, query, pages, *projections)
+    )(meta, query, projections, *pages)
 
     got = sent(send, "c", NC, 1)
     part_type = jax.ShapeDtypeStruct((rows + TAIL, 2 * DV), BF16)
@@ -393,17 +481,16 @@
         compiler_params=small,
         name="heads",
     )(chip[0], *[sent(chip[k], "x", NX, k) for k in range(1, NX)])
-    near = [heads] + [sent(heads, "x", NX, k) for k in range(1, NX)]
-    far = sent(jnp.stack(near), "c", NC, 1)
+    near, far = gathered(heads)
 
     mixed = pl.pallas_call(
         output_kernel,
-        out_shape=jax.ShapeDtypeStruct((weights[0].shape[0], rows), BF16),
-        in_specs=[spec(VMEM)] * (NXC + NX + 1),
+        out_shape=jax.ShapeDtypeStruct((w_o.shape[1] // NXC, rows), BF16),
+        in_specs=[spec(VMEM)] * (NX + 2),
         out_specs=spec(VMEM),
         compiler_params=small,
         name="output",
-    )(*weights, *near, far)
+    )(weights, *near, far)
     mixed = lax.all_to_all(mixed, "z", split_axis=0, concat_axis=0, tiled=True)
     mixed = mixed.reshape(NZ, -1, rows).astype(F32).sum(axis=0)
     return mixed.T.astype(BF16)

time: 219 us -> 157 us (0.72)
  waiting for transfers between devices: 85.8 us -> 35.4 us
  local copies, waits for them, and re-layouts: 26.4 us -> 10.9 us
  other arithmetic: 1.4 us -> 5.3 us
  Pallas kernels: 22.8 us -> 26.6 us
  blocking collectives: 23.3 us -> 21 us
    ppermute x29 -> x16, waiting for transfers between devices: 84.1 us -> 24.1 us  [sent(): return lax.ppermute(x, axis, [(i, i ^ k) for i in range(size)])]
    unnamed x63 -> x11, local copies, waits for them, and re-layouts: 22.4 us -> 5.07 us
    ppermute x0 -> x8, starting transfers between devices: none -> 15.6 us  [shifted(): return lax.ppermute(x, 'z', [(i, (i + k) % NZ) for i in range(NZ)])]
    ppermute x29 -> x16, starting transfers between devices: 38.1 us -> 23.1 us  [sent(): return lax.ppermute(x, axis, [(i, i ^ k) for i in range(size)])]
    ppermute x0 -> x8, waiting for transfers between devices: none -> 7.25 us  [shifted(): return lax.ppermute(x, 'z', [(i, (i + k) % NZ) for i in range(NZ)])]
    pallas_call x1, Pallas kernels: 1.26 us -> 4.12 us  [local(): pl.pallas_call(query_kernel, out_shape=jax.ShapeDtypeStruct((per_group, N...]
    another operation x1 -> x4, other arithmetic: 0.07 us -> 2.67 us  [the longest x1 1.39 us: local(): jnp.stack([sent(part, 'x', NX, k) if k else part for k, part in enumerate...]
    ppermute x3, waiting for transfers between devices: 1.72 us -> 4.09 us  [local(): lax.ppermute(packed[k], 'grp', [(i, (i + k) % groups) for i in range(grou...]
  transfers between devices with their start and end apart: 33 -> 29, of which waited for: 22 -> 13; matrix products, arithmetic and copies ran while one was open for 5% -> 7% of each run, Pallas kernels for 1% -> 16%
where the time goes in v3:
time: 157 us
  starting transfers between devices  43.9 us (28%)
  waiting for transfers between devices  35.4 us (23%)
  Pallas kernels  26.6 us (17%)
  blocking collectives  21 us (13%)
  between operations  13.6 us (9%)
  local copies, waits for them, and re-layouts  10.9 us (7%)
  other arithmetic  5.3 us (3%)
    ppermute x16, waiting for transfers between devices, sent(): return lax.ppermute(x, axis, [(i, i ^ k) for i in range(size)])  24.1 us
    ppermute x16, starting transfers between devices, sent(): return lax.ppermute(x, axis, [(i, i ^ k) for i in range(size)])  23.1 us
    all_to_all x1, blocking collectives, local(): mixed = lax.all_to_all(mixed, 'z', split_axis=0, concat_axis=0, tiled=True)  21 us
    ppermute x8, starting transfers between devices, shifted(): return lax.ppermute(x, 'z', [(i, (i + k) % NZ) for i in range(NZ)])  15.6 us
    pallas_call x1, Pallas kernels, local(): pl.pallas_call(functools.partial(attention_kernel, scale=scale), out_shap...  14.2 us
    ppermute x8, waiting for transfers between devices, shifted(): return lax.ppermute(x, 'z', [(i, (i + k) % NZ) for i in range(NZ)])  7.25 us
    ppermute x3, starting transfers between devices, local(): lax.ppermute(packed[k], 'grp', [(i, (i + k) % groups) for i in range(grou...  5.14 us
    unnamed x11, local copies, waits for them, and re-layouts  5.07 us
  transfers between devices with their start and end apart: 29, of which 13 were waited for; matrix products, arithmetic and copies ran while one was open for 7% of the time, Pallas kernels for 16%

profile of v3, /device:TPU:1, one launch (start us, length us, event | category | flops | bytes accessed | tf_op | source)
XLA Modules:
  0.0 156.7 jit_solution(15487903513532607960)
XLA Ops:
  6.5 1.9 %pad_maximum_fusion.3 = bf16[512,512]{1,0:T(8,128)(2,1)} fusion(bf16[512,256]{1,0:T(8,128)(2,1)} %param.16, bf16[512,256]{1,0:T(8,128)(2,1)} %param.15), kind=kLoop, calls=%fused_computation.3 | loop fusion | flops 1048576 | bytes 1048576 | tf_op jit(solution)/shard_map/concatenate | solution.py:364
  8.6 4.8 %prepare.1 = (s32[41]{0:T(128)S(1)}, bf16[256,384]{1,0:T(8,128)(2,1)S(1)}, bf16[288,512]{1,0:T(8,128)(2,1)S(1)}, bf16[288,512]{1,0:T(8,128)(2,1)S(1)}, bf16[288,...) custom-call(s32[2]{0:T(128)S(1)} %pad_add_fusion.ids, s32[8,64]{1,0:T(8,128)} %bitcast.52, s32[64]{0:T(128)} %refs_1_.1, ...), custom_call_target="tpu_custom_call" | custom-call | tf_op jit(solution)/shard_map/prepare/pallas_call | solution.py:368
  13.3 2.1 %collective-permute-start.3 = (bf16[256,384]{1,0:T(8,128)(2,1)S(1)}, bf16[256,384]{1,0:T(8,128)(2,1)S(1)}, u32[]{:S(2)}, u32[]{:S(2)}) collective-permute-start(bf16[256,384]{1,0:T(8,128)(2,1)S(1)} %get-tuple-element.57.refs_0_), channel_id=1, source_target_pairs={{0,2},{2,0},{4,6},{6,4},{1,3},{3,1},{5,7},{7,5},{8,10},{10,8},{12,... | collective-permute-start | bytes 589832 | tf_op jit(solution)/shard_map/ppermute | solution.py:324
  15.5 2.5 %collective-permute-start.4 = (bf16[256,384]{1,0:T(8,128)(2,1)S(1)}, bf16[256,384]{1,0:T(8,128)(2,1)S(1)}, u32[]{:S(2)}, u32[]{:S(2)}) collective-permute-start(bf16[256,384]{1,0:T(8,128)(2,1)S(1)} %get-tuple-element.57.refs_0_), channel_id=1, source_target_pairs={{0,4},{2,6},{4,0},{6,2},{1,5},{3,7},{5,1},{7,3},{8,12},{10,14},{12... | collective-permute-start | bytes 589832 | tf_op jit(solution)/shard_map/ppermute | solution.py:324
  19.4 2.6 %collective-permute-start.1 = (bf16[288,512]{1,0:T(8,128)(2,1)S(1)}, bf16[288,512]{1,0:T(8,128)(2,1)S(1)}, u32[]{:S(2)}, u32[]{:S(2)}) collective-permute-start(bf16[288,512]{1,0:T(8,128)(2,1)S(1)} %get-tuple-element.39), channel_id=1, source_target_pairs={{0,128},{64,192},{128,0},{192,64},{1,129},{65,193},{129,1},{193,65... | collective-permute-start | bytes 884744 | tf_op jit(solution)/shard_map/ppermute | solution.py:393
  23.1 2.2 %constant_dynamic-slice_fusion.1 = bf16[256,1792]{1,0:T(8,128)(2,1)} fusion(bf16[256,7168]{1,0:T(8,128)(2,1)} %param.17, s32[]{:T(128)S(6)} %select_n.37), kind=kLoop, calls=%fused_computation.11 | loop fusion | bytes 1835012 | tf_op jit(solution)/shard_map/dynamic_slice | solution.py:400
  25.3 2.2 %copy.14 = bf16[256,1792]{0,1:T(8,128)(2,1)} copy(bf16[256,1792]{1,0:T(8,128)(2,1)} %constant_dynamic-slice_fusion.1) | data formatting | bytes 1835008
  27.5 2.2 %dynamic-slice_bitcast_fusion.1 = (bf16[2,2,112,256]{3,2,1,0:T(8,128)(2,1)}, bf16[2,2,112,256]{3,2,1,0:T(8,128)(2,1)}, bf16[2,2,112,256]{3,2,1,0:T(8,128)(2,1)}, bf16[2,2,112,256]{3,2,1,0:T(8,128)(2,1)}) fusion(bf16[2,4,2,112,256]{4,3,2,1,0:T(8,128)(2,1)} %bitcast.46, s32[]{:T(128)S(6)} %select_n.42, s32[]{:T(128)S(6)} %select_n.41, s32[]{:T(128)S(6)} %select_n.40, ...), kind=kLoop, calls=%fused_computation.6 | loop fusion | bytes 1835024 | tf_op jit(solution)/shard_map/jit(dynamic_index_in_dim)/squeeze | solution.py:403
  29.8 4.1 %collective-permute-done.1.rest_2_ = bf16[288,512]{1,0:T(8,128)(2,1)S(1)} collective-permute-done((bf16[288,512]{1,0:T(8,128)(2,1)S(1)}, bf16[288,512]{1,0:T(8,128)(2,1)S(1)}, u32[]{:S(2)}, u32[]{:S(2)}) %collective-permute-start.1) | collective-permute-done | bytes 294944 | tf_op jit(solution)/shard_map/ppermute | solution.py:393
  34.5 1.7 %collective-permute-start.11 = (bf16[288,512]{1,0:T(8,128)(2,1)S(1)}, bf16[288,512]{1,0:T(8,128)(2,1)S(1)}, u32[]{:S(2)}, u32[]{:S(2)}) collective-permute-start(bf16[288,512]{1,0:T(8,128)(2,1)S(1)} %pick.1.rest_0_), channel_id=1, source_target_pairs={{0,8},{8,16},{16,24},{24,32},{32,40},{40,48},{48,56},{56,0},{1,9},... | collective-permute-start | bytes 884744 | tf_op jit(solution)/shard_map/ppermute | solution.py:333
  36.2 4.0 %collective-permute-start.9 = (bf16[288,512]{1,0:T(8,128)(2,1)S(1)}, bf16[288,512]{1,0:T(8,128)(2,1)S(1)}, u32[]{:S(2)}, u32[]{:S(2)}) collective-permute-start(bf16[288,512]{1,0:T(8,128)(2,1)S(1)} %pick.1.rest_0_), channel_id=1, source_target_pairs={{0,56},{8,0},{16,8},{24,16},{32,24},{40,32},{48,40},{56,48},{1,57}... | collective-permute-start | bytes 884744 | tf_op jit(solution)/shard_map/ppermute | solution.py:333
  40.2 3.7 %collective-permute-start.7 = (bf16[2,2,112,256]{3,2,1,0:T(8,128)(2,1)}, bf16[2,2,112,256]{3,2,1,0:T(8,128)(2,1)S(1)}, u32[]{:S(2)}, u32[]{:S(2)}) collective-permute-start(bf16[2,2,112,256]{3,2,1,0:T(8,128)(2,1)} %get-tuple-element.52), channel_id=1, source_target_pairs={{0,4},{2,6},{4,0},{6,2},{1,5},{3,7},{5,1},{7,3},{8,12},{10,14},{12... | collective-permute-start | bytes 688136 | tf_op jit(solution)/shard_map/ppermute | solution.py:324
  45.1 2.7 %collective-permute-start.10 = (bf16[288,512]{1,0:T(8,128)(2,1)S(1)}, bf16[288,512]{1,0:T(8,128)(2,1)S(1)}, u32[]{:S(2)}, u32[]{:S(2)}) collective-permute-start(bf16[288,512]{1,0:T(8,128)(2,1)S(1)} %collective-permute-done.9.rest_1_), channel_id=1, source_target_pairs={{0,56},{8,0},{16,8},{24,16},{32,24},{40,32},{48,40},{56,48},{1,57}... | collective-permute-start | bytes 884744 | tf_op jit(solution)/shard_map/ppermute | solution.py:333
  47.8 1.6 collective-permute-done.6
  49.3 5.2 %collective-permute-done.7 = bf16[2,2,112,256]{3,2,1,0:T(8,128)(2,1)S(1)} collective-permute-done((bf16[2,2,112,256]{3,2,1,0:T(8,128)(2,1)}, bf16[2,2,112,256]{3,2,1,0:T(8,128)(2,1)S(1)}, u32[]{:S(2)}, u32[]{:S(2)}) %collective-permute-start.7) | collective-permute-done | bytes 229408 | tf_op jit(solution)/shard_map/ppermute | solution.py:324
  56.8 3.9 %collective-permute-start.13 = (bf16[4,2,112,256]{3,2,1,0:T(8,128)(2,1)S(1)}, bf16[4,2,112,256]{3,2,1,0:T(8,128)(2,1)S(1)}, u32[]{:S(2)}, u32[]{:S(2)}) collective-permute-start(bf16[4,2,112,256]{3,2,1,0:T(8,128)(2,1)S(1)} %get-tuple-element.68), channel_id=1, source_target_pairs={{0,1},{1,0},{2,3},{3,2},{4,5},{5,4},{6,7},{7,6},{8,9},{9,8},{10,11... | collective-permute-start | bytes 1376264 | tf_op jit(solution)/shard_map/ppermute | solution.py:324
  61.3 3.9 %collective-permute-start.14 = (bf16[288,512]{1,0:T(8,128)(2,1)S(1)}, bf16[288,512]{1,0:T(8,128)(2,1)S(1)}, u32[]{:S(2)}, u32[]{:S(2)}) collective-permute-start(bf16[288,512]{1,0:T(8,128)(2,1)S(1)} %collective-permute-done.10.rest_2_), channel_id=1, source_target_pairs={{0,56},{8,0},{16,8},{24,16},{32,24},{40,32},{48,40},{56,48},{1,57}... | collective-permute-start | bytes 884744 | tf_op jit(solution)/shard_map/ppermute | solution.py:333
  66.3 6.2 %collective-permute-done.15.rest_5_ = bf16[288,512]{1,0:T(8,128)(2,1)S(1)} collective-permute-done((bf16[288,512]{1,0:T(8,128)(2,1)S(1)}, bf16[288,512]{1,0:T(8,128)(2,1)S(1)}, u32[]{:S(2)}, u32[]{:S(2)}) %collective-permute-start.15) | collective-permute-done | bytes 294944 | tf_op jit(solution)/shard_map/ppermute | solution.py:333
  74.7 2.7 %collective-permute-start.18 = (bf16[144,512]{1,0:T(8,128)(2,1)}, bf16[144,512]{1,0:T(8,128)(2,1)}, u32[]{:S(2)}, u32[]{:S(2)}) collective-permute-start(bf16[144,512]{1,0:T(8,128)(2,1)} %slice.9), channel_id=1, source_target_pairs={{0,56},{8,0},{16,8},{24,16},{32,24},{40,32},{48,40},{56,48},{1,57}... | collective-permute-start | bytes 442376 | tf_op jit(solution)/shard_map/ppermute | solution.py:333
  77.4 4.1 %query.1 = bf16[8,512,640]{2,1,0:T(8,128)(2,1)S(1)} custom-call(s32[41]{0:T(128)S(1)} %get-tuple-element.36.meta, bf16[256,384]{1,0:T(8,128)(2,1)S(1)} %get-tuple-element.57.refs_0_, bf16[256,384]{1,0:T(8,128)(2,1)S(1)} %collective-permute-done.3.refs_1_, bf16[256,384]{1,0:T(8,128)(2,1)S(1)} %collective-permute-done.4.refs_2_, ...), custom_call_target="tpu_custom_call" | custom-call | tf_op jit(solution)/shard_map/query/pallas_call | solution.py:434
  81.6 14.2 %attention.1 = (bf16[4,272,256]{2,1,0:T(8,128)(2,1)S(1)}, bf16[4,272,256]{2,1,0:T(8,128)(2,1)S(1)}) custom-call(s32[41]{0:T(128)S(1)} %get-tuple-element.36.meta, bf16[8,512,640]{2,1,0:T(8,128)(2,1)S(1)} %query.1, bf16[8,512,512]{2,1,0:T(8,128)(2,1)} %bitcast.45, bf16[288,512]{1,0:T(8,128)(2,1)S(1)} %pick.1.rest_0_, ...), custom_call_target="tpu_custom_call" | custom-call | tf_op jit(solution)/shard_map/attention/pallas_call | solution.py:448
  96.5 1.6 %collective-permute-done.19.got = bf16[4,272,256]{2,1,0:T(8,128)(2,1)S(1)} collective-permute-done((bf16[4,272,256]{2,1,0:T(8,128)(2,1)S(1)}, bf16[4,272,256]{2,1,0:T(8,128)(2,1)S(1)}, u32[]{:S(2)}, u32[]{:S(2)}) %collective-permute-start.19) | collective-permute-done | bytes 557088 | tf_op jit(solution)/shard_map/ppermute | solution.py:324
  99.2 3.7 %collective-permute-start.22 = (bf16[272,256]{1,0:T(8,128)(2,1)S(1)}, bf16[272,256]{1,0:T(8,128)(2,1)S(1)}, u32[]{:S(2)}, u32[]{:S(2)}) collective-permute-start(bf16[272,256]{1,0:T(8,128)(2,1)S(1)} %get-tuple-element.66), channel_id=1, source_target_pairs={{0,6},{2,4},{4,2},{6,0},{1,7},{3,5},{5,3},{7,1},{8,14},{10,12},{12... | collective-permute-start | bytes 417800 | tf_op jit(solution)/shard_map/ppermute | solution.py:324
  104.1 1.5 collective-permute-done.21.refs_2_
  105.6 3.8 %collective-permute-done.22.refs_3_ = bf16[272,256]{1,0:T(8,128)(2,1)S(1)} collective-permute-done((bf16[272,256]{1,0:T(8,128)(2,1)S(1)}, bf16[272,256]{1,0:T(8,128)(2,1)S(1)}, u32[]{:S(2)}, u32[]{:S(2)}) %collective-permute-start.22) | collective-permute-done | bytes 139296 | tf_op jit(solution)/shard_map/ppermute | solution.py:324
  110.0 3.8 %collective-permute-start.24 = (bf16[256,256]{1,0:T(8,128)(2,1)S(1)}, bf16[256,256]{1,0:T(8,128)(2,1)S(1)}, u32[]{:S(2)}, u32[]{:S(2)}) collective-permute-start(bf16[256,256]{1,0:T(8,128)(2,1)S(1)} %heads.1.refs_0_), channel_id=1, source_target_pairs={{0,4},{2,6},{4,0},{6,2},{1,5},{3,7},{5,1},{7,3},{8,12},{10,14},{12... | collective-permute-start | bytes 393224 | tf_op jit(solution)/shard_map/ppermute | solution.py:324
  114.8 4.0 %collective-permute-done.24.refs_2_ = bf16[256,256]{1,0:T(8,128)(2,1)S(1)} collective-permute-done((bf16[256,256]{1,0:T(8,128)(2,1)S(1)}, bf16[256,256]{1,0:T(8,128)(2,1)S(1)}, u32[]{:S(2)}, u32[]{:S(2)}) %collective-permute-start.24) | collective-permute-done | bytes 131104 | tf_op jit(solution)/shard_map/ppermute | solution.py:324
  118.8 2.8 %collective-permute-done.25.refs_3_ = bf16[256,256]{1,0:T(8,128)(2,1)S(1)} collective-permute-done((bf16[256,256]{1,0:T(8,128)(2,1)S(1)}, bf16[256,256]{1,0:T(8,128)(2,1)S(1)}, u32[]{:S(2)}, u32[]{:S(2)}) %collective-permute-start.25) | collective-permute-done | bytes 131104 | tf_op jit(solution)/shard_map/ppermute | solution.py:324
  121.7 1.5 collective-permute-start.26
  123.2 1.5 collective-permute-done.26.refs_4_
  124.7 2.0 %copy-done = bf16[8,4,224,256]{3,2,1,0:T(8,128)(2,1)S(1)} copy-done((bf16[8,4,224,256]{3,2,1,0:T(8,128)(2,1)S(1)}, bf16[8,4,224,256]{3,2,1,0:T(8,128)(2,1)}, u32[]{:S(2)}) %copy-start) | copy-done | bytes 3670040
  128.2 21.0 %all_to_all.9 = bf16[8,112,256]{2,1,0:T(8,128)(2,1)S(1)} all-to-all(bf16[8,112,256]{2,1,0:T(8,128)(2,1)S(1)} %bitcast.35), channel_id=1, replica_groups=mesh['grp'=4,'z'=8,'x'=4,'c'=2] {'z'}, dimensions={0} | all-to-all | bytes 917504 | tf_op jit(solution)/shard_map/all_to_all | solution.py:494
  (59 shorter events, 17.4 us)
Async XLA Ops:
  6.5 70.9 %all-gather.7.cloned.1.call-start = ((), (), s32[]{:S(2)}) async-start(), calls=%async_computation.2 | async-start | bytes 4718592 | tf_op jit(solution)/shard_map/all_gather | solution.py:364
  8.4 114.8 %all-gather.5.cloned.1.call-start = ((), (), s32[]{:S(2)}) async-start(), calls=%async_computation.1 | async-start | bytes 4587520 | tf_op jit(solution)/shard_map/all_gather | solution.py:432
  13.3 8.7 %collective-permute-start.3 = (bf16[256,384]{1,0:T(8,128)(2,1)S(1)}, bf16[256,384]{1,0:T(8,128)(2,1)S(1)}, u32[]{:S(2)}, u32[]{:S(2)}) collective-permute-start(bf16[256,384]{1,0:T(8,128)(2,1)S(1)} %get-tuple-element.57.refs_0_), channel_id=1, source_target_pairs={{0,2},{2,0},{4,6},{6,4},{1,3},{3,1},{5,7},{7,5},{8,10},{10,8},{12,... | collective-permute-start | bytes 589832 | tf_op jit(solution)/shard_map/ppermute | solution.py:324
  15.5 14.3 %collective-permute-start.4 = (bf16[256,384]{1,0:T(8,128)(2,1)S(1)}, bf16[256,384]{1,0:T(8,128)(2,1)S(1)}, u32[]{:S(2)}, u32[]{:S(2)}) collective-permute-start(bf16[256,384]{1,0:T(8,128)(2,1)S(1)} %get-tuple-element.57.refs_0_), channel_id=1, source_target_pairs={{0,4},{2,6},{4,0},{6,2},{1,5},{3,7},{5,1},{7,3},{8,12},{10,14},{12... | collective-permute-start | bytes 589832 | tf_op jit(solution)/shard_map/ppermute | solution.py:324
  17.9 11.8 %collective-permute-start.5 = (bf16[256,384]{1,0:T(8,128)(2,1)S(1)}, bf16[256,384]{1,0:T(8,128)(2,1)S(1)}, u32[]{:S(2)}, u32[]{:S(2)}) collective-permute-start(bf16[256,384]{1,0:T(8,128)(2,1)S(1)} %get-tuple-element.57.refs_0_), channel_id=1, source_target_pairs={{0,6},{2,4},{4,2},{6,0},{1,7},{3,5},{5,3},{7,1},{8,14},{10,12},{12... | collective-permute-start | bytes 589832 | tf_op jit(solution)/shard_map/ppermute | solution.py:324
  18.0 11.8 %collective-permute-start = (bf16[288,512]{1,0:T(8,128)(2,1)S(1)}, bf16[288,512]{1,0:T(8,128)(2,1)S(1)}, u32[]{:S(2)}, u32[]{:S(2)}) collective-permute-start(bf16[288,512]{1,0:T(8,128)(2,1)S(1)} %get-tuple-element.38), channel_id=1, source_target_pairs={{0,64},{64,128},{128,192},{192,0},{1,65},{65,129},{129,193},{193,1... | collective-permute-start | bytes 884744 | tf_op jit(solution)/shard_map/ppermute | solution.py:393
  19.4 14.5 %collective-permute-start.1 = (bf16[288,512]{1,0:T(8,128)(2,1)S(1)}, bf16[288,512]{1,0:T(8,128)(2,1)S(1)}, u32[]{:S(2)}, u32[]{:S(2)}) collective-permute-start(bf16[288,512]{1,0:T(8,128)(2,1)S(1)} %get-tuple-element.39), channel_id=1, source_target_pairs={{0,128},{64,192},{128,0},{192,64},{1,129},{65,193},{129,1},{193,65... | collective-permute-start | bytes 884744 | tf_op jit(solution)/shard_map/ppermute | solution.py:393
  22.0 11.8 %collective-permute-start.2 = (bf16[288,512]{1,0:T(8,128)(2,1)S(1)}, bf16[288,512]{1,0:T(8,128)(2,1)S(1)}, u32[]{:S(2)}, u32[]{:S(2)}) collective-permute-start(bf16[288,512]{1,0:T(8,128)(2,1)S(1)} %get-tuple-element.40), channel_id=1, source_target_pairs={{0,192},{64,0},{128,64},{192,128},{1,193},{65,1},{129,65},{193,129... | collective-permute-start | bytes 884744 | tf_op jit(solution)/shard_map/ppermute | solution.py:393
  34.5 10.6 %collective-permute-start.11 = (bf16[288,512]{1,0:T(8,128)(2,1)S(1)}, bf16[288,512]{1,0:T(8,128)(2,1)S(1)}, u32[]{:S(2)}, u32[]{:S(2)}) collective-permute-start(bf16[288,512]{1,0:T(8,128)(2,1)S(1)} %pick.1.rest_0_), channel_id=1, source_target_pairs={{0,8},{8,16},{16,24},{24,32},{32,40},{40,48},{48,56},{56,0},{1,9},... | collective-permute-start | bytes 884744 | tf_op jit(solution)/shard_map/ppermute | solution.py:333
  36.2 8.9 %collective-permute-start.9 = (bf16[288,512]{1,0:T(8,128)(2,1)S(1)}, bf16[288,512]{1,0:T(8,128)(2,1)S(1)}, u32[]{:S(2)}, u32[]{:S(2)}) collective-permute-start(bf16[288,512]{1,0:T(8,128)(2,1)S(1)} %pick.1.rest_0_), channel_id=1, source_target_pairs={{0,56},{8,0},{16,8},{24,16},{32,24},{40,32},{48,40},{56,48},{1,57}... | collective-permute-start | bytes 884744 | tf_op jit(solution)/shard_map/ppermute | solution.py:333
  40.2 9.1 %collective-permute-start.6 = (bf16[2,2,112,256]{3,2,1,0:T(8,128)(2,1)}, bf16[2,2,112,256]{3,2,1,0:T(8,128)(2,1)}, u32[]{:S(2)}, u32[]{:S(2)}) collective-permute-start(bf16[2,2,112,256]{3,2,1,0:T(8,128)(2,1)} %get-tuple-element.51), channel_id=1, source_target_pairs={{0,2},{2,0},{4,6},{6,4},{1,3},{3,1},{5,7},{7,5},{8,10},{10,8},{12,... | collective-permute-start | bytes 688136 | tf_op jit(solution)/shard_map/ppermute | solution.py:324
  40.2 14.3 %collective-permute-start.7 = (bf16[2,2,112,256]{3,2,1,0:T(8,128)(2,1)}, bf16[2,2,112,256]{3,2,1,0:T(8,128)(2,1)S(1)}, u32[]{:S(2)}, u32[]{:S(2)}) collective-permute-start(bf16[2,2,112,256]{3,2,1,0:T(8,128)(2,1)} %get-tuple-element.52), channel_id=1, source_target_pairs={{0,4},{2,6},{4,0},{6,2},{1,5},{3,7},{5,1},{7,3},{8,12},{10,14},{12... | collective-permute-start | bytes 688136 | tf_op jit(solution)/shard_map/ppermute | solution.py:324
  43.9 10.6 %collective-permute-start.8 = (bf16[2,2,112,256]{3,2,1,0:T(8,128)(2,1)}, bf16[2,2,112,256]{3,2,1,0:T(8,128)(2,1)S(1)}, u32[]{:S(2)}, u32[]{:S(2)}) collective-permute-start(bf16[2,2,112,256]{3,2,1,0:T(8,128)(2,1)} %get-tuple-element.53), channel_id=1, source_target_pairs={{0,6},{2,4},{4,2},{6,0},{1,7},{3,5},{5,3},{7,1},{8,14},{10,12},{12... | collective-permute-start | bytes 688136 | tf_op jit(solution)/shard_map/ppermute | solution.py:324
  45.1 11.6 %collective-permute-start.12 = (bf16[288,512]{1,0:T(8,128)(2,1)S(1)}, bf16[288,512]{1,0:T(8,128)(2,1)S(1)}, u32[]{:S(2)}, u32[]{:S(2)}) collective-permute-start(bf16[288,512]{1,0:T(8,128)(2,1)S(1)} %collective-permute-done.11.rest_7_), channel_id=1, source_target_pairs={{0,8},{8,16},{16,24},{24,32},{32,40},{40,48},{48,56},{56,0},{1,9},... | collective-permute-start | bytes 884744 | tf_op jit(solution)/shard_map/ppermute | solution.py:333
  45.1 11.6 %collective-permute-start.10 = (bf16[288,512]{1,0:T(8,128)(2,1)S(1)}, bf16[288,512]{1,0:T(8,128)(2,1)S(1)}, u32[]{:S(2)}, u32[]{:S(2)}) collective-permute-start(bf16[288,512]{1,0:T(8,128)(2,1)S(1)} %collective-permute-done.9.rest_1_), channel_id=1, source_target_pairs={{0,56},{8,0},{16,8},{24,16},{32,24},{40,32},{48,40},{56,48},{1,57}... | collective-permute-start | bytes 884744 | tf_op jit(solution)/shard_map/ppermute | solution.py:333
  56.7 15.8 %copy-start.1 = (bf16[288,512]{1,0:T(8,128)(2,1)}, bf16[288,512]{1,0:T(8,128)(2,1)S(1)}, u32[]{:S(2)}) copy-start(bf16[288,512]{1,0:T(8,128)(2,1)S(1)} %collective-permute-done.10.rest_2_) | copy-start | bytes 884740
  56.8 8.4 %collective-permute-start.13 = (bf16[4,2,112,256]{3,2,1,0:T(8,128)(2,1)S(1)}, bf16[4,2,112,256]{3,2,1,0:T(8,128)(2,1)S(1)}, u32[]{:S(2)}, u32[]{:S(2)}) collective-permute-start(bf16[4,2,112,256]{3,2,1,0:T(8,128)(2,1)S(1)} %get-tuple-element.68), channel_id=1, source_target_pairs={{0,1},{1,0},{2,3},{3,2},{4,5},{5,4},{6,7},{7,6},{8,9},{9,8},{10,11... | collective-permute-start | bytes 1376264 | tf_op jit(solution)/shard_map/ppermute | solution.py:324
  60.7 11.8 %collective-permute-start.15 = (bf16[288,512]{1,0:T(8,128)(2,1)S(1)}, bf16[288,512]{1,0:T(8,128)(2,1)S(1)}, u32[]{:S(2)}, u32[]{:S(2)}) collective-permute-start(bf16[288,512]{1,0:T(8,128)(2,1)S(1)} %collective-permute-done.12.rest_6_), channel_id=1, source_target_pairs={{0,8},{8,16},{16,24},{24,32},{32,40},{40,48},{48,56},{56,0},{1,9},... | collective-permute-start | bytes 884744 | tf_op jit(solution)/shard_map/ppermute | solution.py:333
  61.3 11.2 %collective-permute-start.14 = (bf16[288,512]{1,0:T(8,128)(2,1)S(1)}, bf16[288,512]{1,0:T(8,128)(2,1)S(1)}, u32[]{:S(2)}, u32[]{:S(2)}) collective-permute-start(bf16[288,512]{1,0:T(8,128)(2,1)S(1)} %collective-permute-done.10.rest_2_), channel_id=1, source_target_pairs={{0,56},{8,0},{16,8},{24,16},{32,24},{40,32},{48,40},{56,48},{1,57}... | collective-permute-start | bytes 884744 | tf_op jit(solution)/shard_map/ppermute | solution.py:333
  72.7 4.8 %collective-permute-start.16 = (bf16[4,256,384]{2,1,0:T(8,128)(2,1)S(1)}, bf16[4,256,384]{2,1,0:T(8,128)(2,1)S(1)}, u32[]{:S(2)}, u32[]{:S(2)}) collective-permute-start(bf16[4,256,384]{2,1,0:T(8,128)(2,1)S(1)} %pad_maximum_fusion.2), channel_id=1, source_target_pairs={{0,1},{1,0},{2,3},{3,2},{4,5},{5,4},{6,7},{7,6},{8,9},{9,8},{10,11... | collective-permute-start | bytes 2359304 | tf_op jit(solution)/shard_map/ppermute | solution.py:324
  74.1 7.5 %collective-permute-start.17 = (bf16[144,512]{1,0:T(8,128)(2,1)}, bf16[144,512]{1,0:T(8,128)(2,1)S(1)}, u32[]{:S(2)}, u32[]{:S(2)}) collective-permute-start(bf16[144,512]{1,0:T(8,128)(2,1)} %slice.8), channel_id=1, source_target_pairs={{0,8},{8,16},{16,24},{24,32},{32,40},{40,48},{48,56},{56,0},{1,9},... | collective-permute-start | bytes 442376 | tf_op jit(solution)/shard_map/ppermute | solution.py:333
  74.7 6.8 %collective-permute-start.18 = (bf16[144,512]{1,0:T(8,128)(2,1)}, bf16[144,512]{1,0:T(8,128)(2,1)}, u32[]{:S(2)}, u32[]{:S(2)}) collective-permute-start(bf16[144,512]{1,0:T(8,128)(2,1)} %slice.9), channel_id=1, source_target_pairs={{0,56},{8,0},{16,8},{24,16},{32,24},{40,32},{48,40},{56,48},{1,57}... | collective-permute-start | bytes 442376 | tf_op jit(solution)/shard_map/ppermute | solution.py:333
  77.4 4.2 %copy-start.2 = (bf16[288,512]{1,0:T(8,128)(2,1)S(1)}, bf16[288,512]{1,0:T(8,128)(2,1)}, u32[]{:S(2)}) copy-start(bf16[288,512]{1,0:T(8,128)(2,1)} %copy-done.1) | copy-start | bytes 884740
  95.8 2.2 %collective-permute-start.19 = (bf16[4,272,256]{2,1,0:T(8,128)(2,1)S(1)}, bf16[4,272,256]{2,1,0:T(8,128)(2,1)S(1)}, u32[]{:S(2)}, u32[]{:S(2)}) collective-permute-start(bf16[4,272,256]{2,1,0:T(8,128)(2,1)S(1)} %get-tuple-element.62), channel_id=1, source_target_pairs={{0,1},{1,0},{2,3},{3,2},{4,5},{5,4},{6,7},{7,6},{8,9},{9,8},{10,11... | collective-permute-start | bytes 1671176 | tf_op jit(solution)/shard_map/ppermute | solution.py:324
  99.0 5.1 %collective-permute-start.20 = (bf16[272,256]{1,0:T(8,128)(2,1)S(1)}, bf16[272,256]{1,0:T(8,128)(2,1)S(1)}, u32[]{:S(2)}, u32[]{:S(2)}) collective-permute-start(bf16[272,256]{1,0:T(8,128)(2,1)S(1)} %get-tuple-element.64), channel_id=1, source_target_pairs={{0,2},{2,0},{4,6},{6,4},{1,3},{3,1},{5,7},{7,5},{8,10},{10,8},{12,... | collective-permute-start | bytes 417800 | tf_op jit(solution)/shard_map/ppermute | solution.py:324
  99.1 6.5 %collective-permute-start.21 = (bf16[272,256]{1,0:T(8,128)(2,1)S(1)}, bf16[272,256]{1,0:T(8,128)(2,1)S(1)}, u32[]{:S(2)}, u32[]{:S(2)}) collective-permute-start(bf16[272,256]{1,0:T(8,128)(2,1)S(1)} %get-tuple-element.65), channel_id=1, source_target_pairs={{0,4},{2,6},{4,0},{6,2},{1,5},{3,7},{5,1},{7,3},{8,12},{10,14},{12... | collective-permute-start | bytes 417800 | tf_op jit(solution)/shard_map/ppermute | solution.py:324
  99.2 10.2 %collective-permute-start.22 = (bf16[272,256]{1,0:T(8,128)(2,1)S(1)}, bf16[272,256]{1,0:T(8,128)(2,1)S(1)}, u32[]{:S(2)}, u32[]{:S(2)}) collective-permute-start(bf16[272,256]{1,0:T(8,128)(2,1)S(1)} %get-tuple-element.66), channel_id=1, source_target_pairs={{0,6},{2,4},{4,2},{6,0},{1,7},{3,5},{5,3},{7,1},{8,14},{10,12},{12... | collective-permute-start | bytes 417800 | tf_op jit(solution)/shard_map/ppermute | solution.py:324
  109.9 4.9 %collective-permute-start.23 = (bf16[256,256]{1,0:T(8,128)(2,1)S(1)}, bf16[256,256]{1,0:T(8,128)(2,1)S(1)}, u32[]{:S(2)}, u32[]{:S(2)}) collective-permute-start(bf16[256,256]{1,0:T(8,128)(2,1)S(1)} %heads.1.refs_0_), channel_id=1, source_target_pairs={{0,2},{2,0},{4,6},{6,4},{1,3},{3,1},{5,7},{7,5},{8,10},{10,8},{12,... | collective-permute-start | bytes 393224 | tf_op jit(solution)/shard_map/ppermute | solution.py:324
  110.0 8.8 %collective-permute-start.24 = (bf16[256,256]{1,0:T(8,128)(2,1)S(1)}, bf16[256,256]{1,0:T(8,128)(2,1)S(1)}, u32[]{:S(2)}, u32[]{:S(2)}) collective-permute-start(bf16[256,256]{1,0:T(8,128)(2,1)S(1)} %heads.1.refs_0_), channel_id=1, source_target_pairs={{0,4},{2,6},{4,0},{6,2},{1,5},{3,7},{5,1},{7,3},{8,12},{10,14},{12... | collective-permute-start | bytes 393224 | tf_op jit(solution)/shard_map/ppermute | solution.py:324
  113.8 7.9 %collective-permute-start.25 = (bf16[256,256]{1,0:T(8,128)(2,1)S(1)}, bf16[256,256]{1,0:T(8,128)(2,1)S(1)}, u32[]{:S(2)}, u32[]{:S(2)}) collective-permute-start(bf16[256,256]{1,0:T(8,128)(2,1)S(1)} %heads.1.refs_0_), channel_id=1, source_target_pairs={{0,6},{2,4},{4,2},{6,0},{1,7},{3,5},{5,3},{7,1},{8,14},{10,12},{12... | collective-permute-start | bytes 393224 | tf_op jit(solution)/shard_map/ppermute | solution.py:324
  121.7 3.0 %collective-permute-start.26 = (bf16[4,256,256]{2,1,0:T(8,128)(2,1)S(1)}, bf16[4,256,256]{2,1,0:T(8,128)(2,1)S(1)}, u32[]{:S(2)}, u32[]{:S(2)}) collective-permute-start(bf16[4,256,256]{2,1,0:T(8,128)(2,1)S(1)} %pad_maximum_fusion.4), channel_id=1, source_target_pairs={{0,1},{1,0},{2,3},{3,2},{4,5},{5,4},{6,7},{7,6},{8,9},{9,8},{10,11... | collective-permute-start | bytes 1572872 | tf_op jit(solution)/shard_map/ppermute | solution.py:324
  124.7 2.0 %copy-start = (bf16[8,4,224,256]{3,2,1,0:T(8,128)(2,1)S(1)}, bf16[8,4,224,256]{3,2,1,0:T(8,128)(2,1)}, u32[]{:S(2)}) copy-start(bf16[8,4,224,256]{3,2,1,0:T(8,128)(2,1)} %all-gather.5.cloned.1.call-done) | copy-start | bytes 11010052
  (2 other events, 1.5 us)
Sparse Core Ops, SparseCore 0:
  9.2 39.6 all-gather.6
  72.6 44.5 all-gather.4
